TPU v7x, 32 devices: a whole 2x2x4 slice. The times are simulated.
32 devices in a mesh: rep: 2 (over x), seq: 8 (over z, y), tp: 2 (over core).
Axes of the slice: x: 2, y: 2, z: 4, core: 2. Of those that a mesh axis runs over, the one named last changes fastest.
Arguments:
- prefill_query: bfloat16 [8192, 2048], P(('rep', 'seq'), 'tp'), parts along dimension 0, may hold values from -50 to 50
- prefill_key: bfloat16 [8192, 512], P(('rep', 'seq'), 'tp'), parts along dimension 0, may hold values from -6 to 6
- prefill_value: bfloat16 [8192, 512], P(('rep', 'seq'), 'tp'), parts along dimension 0, may hold values from -6 to 6
- doc_ids: int32 [8192], P('rep'), parts along dimension 0, may hold values from 0 to 3, never falling along the last dimension, each value on 1 to 2048 neighbouring positions
- head_window: int32 [16], P('tp'), may hold values from 1024 to 4096, as said below
- dec_query: bfloat16 [128, 2048], P('rep', 'tp'), parts along dimension 0, may hold values from -50 to 50
- dec_key: bfloat16 [128, 512], P('rep', 'tp'), parts along dimension 0, may hold values from -6 to 6
- dec_value: bfloat16 [128, 512], P('rep', 'tp'), parts along dimension 0, may hold values from -6 to 6
- cache_key: bfloat16 [65536, 512], P(('rep', 'seq'), 'tp'), parts along dimension 0, may hold values from -6 to 6
- cache_value: bfloat16 [65536, 512], P(('rep', 'seq'), 'tp'), parts along dimension 0, may hold values from -6 to 6
- page_order: int32 [512], P(('rep', 'seq')), parts along dimension 0, may hold values from 0 to 255, each once
- lengths: int32 [128], P('rep'), parts along dimension 0, may hold values from 1 to 512, 16384 in all
- out_proj: bfloat16 [2048, 4096], P('tp'), may hold values from -0.125 to 0.125
Outputs:
- prompt_out: bfloat16 [8192, 4096], P(('rep', 'seq', 'tp')), parts along dimension 0
- decode_out: bfloat16 [128, 4096], P(('rep', 'tp')), parts along dimension 0
There are 2 independent parts, one for each index of `rep`. A program takes and returns all parts, laid end to end along the dimension named above; an argument that names none is the same for every part. Nothing has to cross between parts.
Inputs may be any that keep to these rules, and one draw needn't show every extreme that they name: `head_window`: some head has window 4096.
All inputs are finite; a program needn't handle non-finite values.
Results may differ from a plain program's by a relative error of at most 0.015.
Values may be sent and summed in bfloat16 or wider, within the bound.
No kernel may reach another device: no remote copies, remote signals or barrier semaphores. Data moves between devices by JAX's collectives and lax.ppermute only.
A program may use at most 256 MiB of HBM per device.

v0:
```python
import math

import jax
import jax.numpy as jnp
from jax import lax
from jax.experimental import pallas as pl
from jax.experimental.pallas import tpu as pltpu
from jax.sharding import PartitionSpec as P


HD = 128
PAGE = 128
NEG = -1e30
FLOOR = -8192.0
SCALE2 = math.log2(math.e) / math.sqrt(HD)
LANES = 128
EXTRA = 16
DOCS = 4
COST = 10**8
CHUNK = 256


VMEM = pl.BlockSpec(memory_space=pltpu.VMEM)
SMEM = pl.BlockSpec(memory_space=pltpu.SMEM)


def scores_of(k, q):
    return (
        lax.dot_general(k, q, (((1,), (1,)), ((), ())), preferred_element_type=jnp.float32) * SCALE2
    )


def flipped(v):
    return jnp.concatenate([v.T, jnp.ones((EXTRA, v.shape[0]), v.dtype)], axis=0)


def doc_starts(doc_ref):
    ids = doc_ref[...]
    return [jnp.sum((ids < d).astype(jnp.int32)) for d in range(1, DOCS)]


def start_at(starts, position):
    start = jnp.zeros_like(position)
    for edge in starts:
        start = jnp.where(position >= edge, edge, start)
    return start


def attend_tile(q, keys, values, state, scratch, i, row_pos, docs, key_pos, win, first, diag, masked):
    m_ref, l_ref, acc_ref = state
    s_ref, p_ref = scratch
    heads = m_ref.shape[1]
    group = heads // len(keys)
    span = keys[0].shape[0]
    chunk = math.gcd(span, CHUNK)
    olds, freshes = {}, {}

    def score(h, c):
        part = slice(c, c + chunk)
        s = scores_of(keys[h // group][part, :], q(slice(h * HD, (h + 1) * HD)))
        if masked:
            if diag:
                allowed = (key_pos[part] >= docs) & (key_pos[part] <= row_pos)
            else:
                allowed = key_pos[part] >= jnp.maximum(docs, row_pos - win[h] + 1)
            s = jnp.where(allowed, s, NEG)
        s_ref[h, part, :] = s
        top = jnp.max(s.reshape(chunk // 8, 8, s.shape[1]), axis=0)
        freshes[h] = top if c == 0 else jnp.maximum(freshes[h], top)
        if c + chunk == span:
            top = jnp.max(freshes[h], axis=0, keepdims=True)
            if not first:
                olds[h] = m_ref[i, h : h + 1, :]
                top = jnp.maximum(olds[h], top)
            freshes[h] = top

    def weigh(h, c):
        part = slice(c, c + chunk)
        p_ref[h, part, :] = jnp.exp2(s_ref[h, part, :] - freshes[h]).astype(jnp.bfloat16)

    def gather(h):
        columns = slice(h * HD, (h + 1) * HD)
        pv = jnp.dot(values[h // group], p_ref[h, :span, :], preferred_element_type=jnp.float32)
        m_ref[i, h : h + 1, :] = freshes[h]
        if first:
            l_ref[i, h : h + 1, :] = pv[HD : HD + 1, :]
            acc_ref[i, columns, :] = pv[:HD, :]
        else:
            shrink = jnp.exp2(olds[h] - freshes[h])
            l_ref[i, h : h + 1, :] = l_ref[i, h : h + 1, :] * shrink + pv[HD : HD + 1, :]
            acc_ref[i, columns, :] = acc_ref[i, columns, :] * shrink + pv[:HD, :]

    for step in range(heads + 2):
        for c in range(0, span, chunk):
            if step < heads:
                score(step, c)
            if 0 <= step - 1 < heads:
                weigh(step - 1, c)
            if step >= 2 and c == 0:
                gather(step - 2)


def own_kernel(win, doc_ref, q_ref, k_ref, v_ref, info_ref, m_ref, l_ref, acc_ref, s_ref, p_ref):
    tiles, _, tq = m_ref.shape
    kv = k_ref.shape[1] // HD
    base = lax.axis_index("seq") * (tiles * tq)
    starts = doc_starts(doc_ref)
    for d, start in enumerate(starts):
        info_ref[d] = start
    for h in range(win.shape[0]):
        info_ref[DOCS - 1 + h] = win[h]
    whole = [flipped(v_ref[:, g * HD : (g + 1) * HD]) for g in range(kv)]
    for i in range(tiles):
        span = (i + 1) * tq
        row_pos = base + i * tq + lax.broadcasted_iota(jnp.int32, (1, tq), 1)
        key_pos = base + lax.broadcasted_iota(jnp.int32, (span, tq), 0)
        keys = [k_ref[:span, g * HD : (g + 1) * HD] for g in range(kv)]
        values = [v[:, :span] for v in whole]
        attend_tile(
            lambda columns, i=i: q_ref[i * tq : (i + 1) * tq, columns],
            keys, values, (m_ref, l_ref, acc_ref), (s_ref, p_ref), i,
            row_pos, start_at(starts, row_pos), key_pos, win, True, True, True,
        )


def far_kernel(info, *refs, sources, last):
    refs = list(refs)
    q_ref = refs[0]
    refs = refs[4:]
    blocks = []
    for distance in sources:
        blocks.append((distance, refs[0], refs[1]))
        refs = refs[2:]
    m_ref, l_ref, acc_ref = refs[:3]
    v_scratch, s_ref, p_ref = refs[-3:]
    out_ref = refs[3]
    tiles, heads, tq = m_ref.shape
    kv = blocks[0][2].shape[1] // HD
    seq = lax.axis_index("seq")
    base = seq * (tiles * tq)
    starts = [info[d] for d in range(DOCS - 1)]
    win = [info[DOCS - 1 + h] for h in range(heads)]
    least, most = win[0], win[0]
    for h in range(1, heads):
        least, most = jnp.minimum(least, win[h]), jnp.maximum(most, win[h])
    for index, (_, _, v_ref) in enumerate(blocks):
        for g in range(kv):
            v_scratch[index, g] = flipped(v_ref[:, g * HD : (g + 1) * HD])

    def q_tile(i, _):
        first_row = base + i * tq
        last_row = first_row + tq - 1
        need_low = jnp.maximum(start_at(starts, first_row), first_row - most + 1)
        full_low = jnp.maximum(start_at(starts, last_row), last_row - least + 1)
        for index, (distance, k_ref, v_ref) in enumerate(blocks):
            span = v_ref.shape[0]
            key_base = base - distance * span
            needed = (key_base >= 0) & (key_base + span - 1 >= need_low)
            full = key_base >= full_low

            def body(masked, index=index, key_base=key_base, k_ref=k_ref, span=span):
                keys = [k_ref[:, g * HD : (g + 1) * HD] for g in range(kv)]
                values = [v_scratch[index, g] for g in range(kv)]
                row_pos = first_row + lax.broadcasted_iota(jnp.int32, (1, tq), 1)
                key_pos = key_base + lax.broadcasted_iota(jnp.int32, (span, tq), 0)
                attend_tile(
                    lambda columns: q_ref[pl.ds(pl.multiple_of(i * tq, tq), tq), columns],
                    keys, values, (m_ref, l_ref, acc_ref), (s_ref, p_ref), i,
                    row_pos, start_at(starts, row_pos) if masked else None, key_pos, win, False, False, masked,
                )

            pl.when(needed & full)(lambda body=body: body(False))
            pl.when(needed & jnp.logical_not(full))(lambda body=body: body(True))
        return 0

    lax.fori_loop(0, tiles, q_tile, 0)
    if last:
        half = lax.axis_index("tp")
        for i in range(tiles):
            place = pl.ds(pl.multiple_of(jnp.where(half == i, tq, 0), tq), tq)
            for h in range(heads):
                columns = slice(h * HD, (h + 1) * HD)
                value = acc_ref[i, columns, :] / l_ref[i, h : h + 1, :]
                out_ref[place, columns] = value.T.astype(jnp.bfloat16)


def decode_kernel(order, lengths, q_ref, ok_ref, ov_ref, k_ref, v_ref, out_ref, s_ref, *, per_request):
    requests = ok_ref.shape[0]
    group = q_ref.shape[1] // HD
    lanes = group * requests
    pages = k_ref.shape[0] // PAGE
    q = jnp.concatenate([q_ref[:, j * HD : (j + 1) * HD] for j in range(group)], axis=0)
    request = jnp.concatenate([lax.broadcasted_iota(jnp.int32, (1, requests), 1)] * group, axis=1)
    place = lax.broadcasted_iota(jnp.int32, (PAGE, lanes), 0)
    own = scores_of(ok_ref[...], q)
    own_row = lax.broadcasted_iota(jnp.int32, (requests, lanes), 0)
    own = jnp.where((own_row == request) & (lax.axis_index("seq") == 0), own, NEG)
    tops = jnp.max(own.reshape(requests // 8, 8, lanes), axis=0)
    for p in range(pages):
        s = scores_of(k_ref[p * PAGE : (p + 1) * PAGE, :], q)
        code = order[p]
        owner = code // per_request
        limit = lengths[owner] - (code - owner * per_request) * PAGE
        s = jnp.where(place < jnp.where(request == owner, limit, 0), s, NEG)
        s_ref[p * PAGE : (p + 1) * PAGE, :] = s
        tops = jnp.maximum(tops, jnp.max(s.reshape(PAGE // 8, 8, lanes), axis=0))
    top = jnp.max(tops, axis=0, keepdims=True)
    top = jnp.maximum(jnp.ceil(top * (1.0 / 32.0)) * 32.0, FLOOR)
    weights = jnp.exp2(s_ref[...] - top).astype(jnp.bfloat16)
    pv = jnp.dot(flipped(v_ref[...]), weights, preferred_element_type=jnp.float32)
    own_weights = jnp.exp2(own - top).astype(jnp.bfloat16)
    pv = pv + jnp.dot(flipped(ov_ref[...]), own_weights, preferred_element_type=jnp.float32)
    out_ref[:HD, :] = pv[:HD, :].astype(jnp.bfloat16)
    out_ref[HD:, :] = packed_stats(top, pv[HD : HD + 1, :])


def packed_stats(top, total):
    high = total.astype(jnp.bfloat16).astype(jnp.float32)
    row = lax.broadcasted_iota(jnp.int32, (EXTRA, top.shape[1]), 0)
    stats = jnp.where(row == 0, top, jnp.where(row == 1, high, total - high))
    return stats.astype(jnp.bfloat16)


def merge_kernel(a_ref, b_ref, out_ref, *, requests, last):
    rows, lanes = a_ref.shape
    kv = rows // (HD + EXTRA)
    group = lanes // requests
    f32 = jnp.float32
    for g in range(kv):
        base = g * (HD + EXTRA)
        body, tile = slice(base, base + HD), slice(base + HD, base + HD + EXTRA)
        left, right = a_ref[tile, :].astype(f32), b_ref[tile, :].astype(f32)
        top = jnp.maximum(left[0:1], right[0:1])
        e1, e2 = jnp.exp2(left[0:1] - top), jnp.exp2(right[0:1] - top)
        total = (left[1:2] + left[2:3]) * e1 + (right[1:2] + right[2:3]) * e2
        value = a_ref[body, :].astype(f32) * e1 + b_ref[body, :].astype(f32) * e2
        if not last:
            out_ref[body, :] = value.astype(jnp.bfloat16)
            out_ref[tile, :] = packed_stats(top, total)
            continue
        value = (value / total).T.astype(jnp.bfloat16)
        per = requests // 2
        half = lax.axis_index("tp")
        for j in range(group):
            columns = slice((g * group + j) * HD, (g * group + j + 1) * HD)
            for part in range(2):
                place = pl.ds(pl.multiple_of(jnp.where(half == part, per, 0), per), per)
                start = j * requests + part * per
                out_ref[place, columns] = value[start : start + per, :]


def product(x, w):
    return jnp.dot(x, w, preferred_element_type=jnp.float32).astype(jnp.bfloat16)


def project_kernel(a_ref, d_ref, w_ref, out_ref, *, column, second):
    x = half_rows(a_ref, d_ref, second)
    step = math.gcd(out_ref.shape[1], 512)
    for c in range(0, out_ref.shape[1], step):
        out_ref[:, c : c + step] = product(x, w_ref[:, column + c : column + c + step])


def half_rows(a_ref, d_ref, second):
    tr, dr = a_ref.shape[0] // 2, d_ref.shape[0] // 2
    return jnp.concatenate(
        [a_ref[second * tr : (second + 1) * tr, :], d_ref[second * dr : (second + 1) * dr, :]], axis=0
    )


def finish_kernel(*refs):
    po_ref, do_ref, s_ref, sems = refs[-4:]
    count = (len(refs) - 4) // 2
    tr = po_ref.shape[0]
    cols = refs[0].shape[1]
    copies = []
    for c in range(count):
        part = slice(c * cols, (c + 1) * cols)
        total = refs[c][...].astype(jnp.float32) + refs[count + c][...].astype(jnp.float32)
        s_ref[:, part] = total.astype(jnp.bfloat16)
        copies.append(pltpu.make_async_copy(s_ref.at[:tr, part], po_ref.at[:, part], sems.at[2 * c]))
        copies.append(pltpu.make_async_copy(s_ref.at[tr:, part], do_ref.at[:, part], sems.at[2 * c + 1]))
        copies[-2].start()
        copies[-1].start()
    for copy in copies:
        copy.wait()


def on_device(
    prefill_query, prefill_key, prefill_value, doc_ids, head_window,
    dec_query, dec_key, dec_value, cache_key, cache_value, page_order, lengths, out_proj,
):
    n = lax.axis_size("seq")
    tokens, width = prefill_query.shape
    kv = prefill_key.shape[1] // HD
    heads = width // HD
    reach = n // 2
    tiles, tq = 2, tokens // 2
    odd = lax.axis_index("seq") % 2
    f32, bf16, i32 = jnp.float32, jnp.bfloat16, jnp.int32

    def ring(x, by):
        return lax.ppermute(x, "seq", [(i, (i + by) % n) for i in range(n)])

    def swap(x, bit=1):
        return lax.ppermute(x, "seq", [(i, i ^ bit) for i in range(n)])

    def pick(even_value, odd_value):
        return jnp.where(odd == 1, odd_value, even_value)

    def params(mib):
        return pltpu.CompilerParams(vmem_limit_bytes=mib << 20)

    def hbm(*arrays):
        return [pltpu.with_memory_space_constraint(x, pltpu.HBM) for x in arrays]

    def cost(us):
        return pl.CostEstimate(flops=int(us * COST), transcendentals=0, bytes_accessed=1 << 20)

    pages = page_order.shape[0]
    requests = dec_query.shape[0]
    group = heads // kv
    tall = HD + EXTRA
    state = [
        jax.ShapeDtypeStruct((tiles, heads, tq), f32),
        jax.ShapeDtypeStruct((tiles, heads, tq), f32),
        jax.ShapeDtypeStruct((tiles, width, tq), f32),
    ]
    pair = [pltpu.VMEM((heads, tokens, tq), f32), pltpu.VMEM((heads, tokens, tq), bf16)]

    def decode_pages(order):
        return pl.pallas_call(
            lambda *refs: decode_kernel(*refs, per_request=pages * n // requests),
            grid=(kv,),
            in_specs=[
                SMEM, SMEM,
                pl.BlockSpec((requests, group * HD), lambda g: (0, g)),
                pl.BlockSpec((requests, HD), lambda g: (0, g)),
                pl.BlockSpec((requests, HD), lambda g: (0, g)),
                pl.BlockSpec((pages * PAGE, HD), lambda g: (0, g)),
                pl.BlockSpec((pages * PAGE, HD), lambda g: (0, g)),
            ],
            out_specs=pl.BlockSpec((tall, group * requests), lambda g: (g, 0)),
            out_shape=jax.ShapeDtypeStruct((kv * tall, group * requests), bf16),
            scratch_shapes=[pltpu.VMEM((pages * PAGE, group * requests), f32)],
            cost_estimate=cost(5),
            compiler_params=params(24),
            name="decode_pages",
        )(*hbm(order, lengths, dec_query, dec_key, dec_value, cache_key, cache_value))

    def merge(partial, other, last):
        return pl.pallas_call(
            lambda *refs: merge_kernel(*refs, requests=requests, last=last),
            in_specs=[VMEM, VMEM],
            out_specs=VMEM,
            out_shape=jax.ShapeDtypeStruct((requests, width) if last else partial.shape, bf16),
            cost_estimate=cost(1),
            compiler_params=params(4),
            name="decode_merge",
        )(partial, other)

    def own(ids):
        return pl.pallas_call(
            own_kernel,
            in_specs=[SMEM] + [VMEM] * 4,
            out_specs=[SMEM] + [VMEM] * 3,
            out_shape=[jax.ShapeDtypeStruct((DOCS - 1 + heads,), i32)] + state,
            scratch_shapes=pair,
            cost_estimate=cost(3),
            compiler_params=params(16),
            name="prompt_own",
        )(*hbm(head_window, ids.reshape(-1, LANES), prefill_query, prefill_key, prefill_value))

    def far(info, carry, stage, last):
        operands = [x for d in stage for x in (keys[d], values[d])]
        scratch = [pltpu.VMEM((len(stage), kv, tall, tokens), bf16)] + pair
        return pl.pallas_call(
            lambda *refs: far_kernel(*refs, sources=stage, last=last),
            in_specs=[SMEM] + [VMEM] * (4 + len(operands)),
            out_specs=[VMEM] * (3 + last),
            out_shape=state + [jax.ShapeDtypeStruct((tokens, width), bf16)] * last,
            input_output_aliases={2: 0, 3: 1, 4: 2},
            scratch_shapes=scratch,
            cost_estimate=cost(5),
            compiler_params=params(20),
            name="prompt_far",
        )(info, prefill_query, *carry, *operands)

    token = [()]

    def then(x):
        x, *token[0] = lax.optimization_barrier((x, *token[0]))
        return x

    def done(*values):
        token[0] = list(values)
        return values if len(values) > 1 else values[0]

    keys, values = {0: prefill_key}, {0: prefill_value}

    def relay(table, d):
        table[d] = done(then(table[d]))
        if d < reach:
            table[d + 2] = ring(table[d], 2)
        fresh = done(pick(table[d - 2], table[d]))
        table[d - 1] = swap(fresh)

    keys[2] = ring(prefill_key, 2)
    info, *carry = done(*own(doc_ids))
    values[2] = ring(then(prefill_value), 2)
    relay(keys, 2)
    partial = done(decode_pages(then(page_order)))
    relay(values, 2)
    other = swap(partial)
    bit = 2

    def step(partial, other, bit):
        partial = done(merge(then(partial), other, bit >= n))
        if bit >= n:
            return partial, None, bit
        return partial, swap(partial, bit), bit * 2

    def attend(d):
        carry[0] = then(carry[0])
        carry[:] = far(info, carry[:3], (d,), d == reach - 1)
        done(carry[0])

    for d in range(4, reach + 1, 2):
        relay(keys, d)
        if bit < n:
            partial, other, bit = step(partial, other, bit)
        relay(values, d)
        attend(d - 2)
        if bit < n:
            partial, other, bit = step(partial, other, bit)
        attend(d - 3)
    attend(reach)
    attend(reach - 1)
    while other is not None:
        partial, other, bit = step(partial, other, bit)
    attn, decode_attn = carry[-1], partial

    model = out_proj.shape[1]
    tr, dr = tokens // 2, requests // 2
    chunks = 2
    cols = model // chunks

    def project(column, second):
        return pl.pallas_call(
            lambda *refs: project_kernel(*refs, column=column, second=second),
            in_specs=[VMEM] * 3,
            out_specs=VMEM,
            out_shape=jax.ShapeDtypeStruct((tr + dr, cols), bf16),
            cost_estimate=cost(2),
            compiler_params=params(16),
            name="project_own" if second else "project_theirs",
        )(attn, decode_attn, out_proj)

    mine, received = [], []
    for c in range(chunks):
        sent = project(c * cols, 0)
        received.append(lax.ppermute(sent, "tp", [(0, 1), (1, 0)]))
        decode_attn = lax.optimization_barrier((decode_attn, sent))[0]
    for c in range(chunks):
        mine.append(project(c * cols, 1))
    return tuple(
        pl.pallas_call(
            finish_kernel,
            in_specs=[VMEM] * (2 * chunks),
            out_specs=[pl.BlockSpec(memory_space=pl.ANY)] * 2,
            out_shape=[jax.ShapeDtypeStruct((tr, model), bf16), jax.ShapeDtypeStruct((dr, model), bf16)],
            scratch_shapes=[pltpu.VMEM((tr + dr, model), bf16), pltpu.SemaphoreType.DMA((2 * chunks,))],
            cost_estimate=cost(3),
            compiler_params=params(12),
            name="project_finish",
        )(*mine, *received)
    )


def solution(mesh):
    placed = (
        P(("rep", "seq"), "tp"),
        P(("rep", "seq"), "tp"),
        P(("rep", "seq"), "tp"),
        P("rep"),
        P("tp"),
        P("rep", "tp"),
        P("rep", "tp"),
        P("rep", "tp"),
        P(("rep", "seq"), "tp"),
        P(("rep", "seq"), "tp"),
        P(("rep", "seq")),
        P("rep"),
        P("tp", None),
    )

    return jax.shard_map(
        on_device,
        mesh=mesh,
        in_specs=placed,
        out_specs=(P(("rep", "seq", "tp"), None), P(("rep", "tp"), None)),
        check_vma=False,
    )
```

profile of v0, /device:TPU:23, one launch (start us, length us, event | category | flops | bytes accessed | tf_op | source)
XLA Modules:
  0.0 58.2 jit_solution(4671081663535228714)
XLA Ops:
  0.6 1.3 %collective-permute-start.1 = (bf16[512,256]{1,0:T(8,128)(2,1)}, bf16[512,256]{1,0:T(8,128)(2,1)S(1)}, u32[]{:S(2)}, u32[]{:S(2)}) collective-permute-start(bf16[512,256]{1,0:T(8,128)(2,1)} %k_ref.1), channel_id=1, source_target_pairs={{0,4},{2,6},{4,8},{6,10},{8,12},{10,14},{12,0},{14,2},{1,5},{3,7},... | collective-permute-start | bytes 786440 | tf_op jit(solution)/shard_map/ppermute | solution.py:302
  2.0 4.0 %prompt_own.1 = (s32[11]{0:T(128)S(1)}, f32[2,8,256]{2,1,0:T(8,128)S(1)}, f32[2,8,256]{2,1,0:T(8,128)S(1)}, f32[2,1024,256]{2,1,0:T(8,128)S(1)}) custom-call(s32[8]{0:T(128)} %win.1, s32[32,128]{1,0:T(8,128)} %bitcast.3, bf16[512,1024]{1,0:T(8,128)(2,1)} %refs_1_.9, bf16[512,256]{1,0:T(8,128)(2,1)} %k_ref.1, bf16[512,256]{1,0:T(8,128)(2,1)} %v_ref.1), custom_call_target="tpu_custom_call" | custom-call | flops 300000000 | bytes 1048576 | tf_op jit(solution)/shard_map/prompt_own/pallas_call | solution.py:362
  6.1 2.0 %collective-permute-done.1.refs_5_ = bf16[512,256]{1,0:T(8,128)(2,1)S(1)} collective-permute-done((bf16[512,256]{1,0:T(8,128)(2,1)}, bf16[512,256]{1,0:T(8,128)(2,1)S(1)}, u32[]{:S(2)}, u32[]{:S(2)}) %collective-permute-start.1) | collective-permute-done | bytes 262176 | tf_op jit(solution)/shard_map/ppermute | solution.py:302
  8.1 1.3 %collective-permute-start.3 = (bf16[512,256]{1,0:T(8,128)(2,1)S(1)}, bf16[512,256]{1,0:T(8,128)(2,1)S(1)}, u32[]{:S(2)}, u32[]{:S(2)}) collective-permute-start(bf16[512,256]{1,0:T(8,128)(2,1)S(1)} %collective-permute-done.1.refs_5_), channel_id=1, source_target_pairs={{0,4},{2,6},{4,8},{6,10},{8,12},{10,14},{12,0},{14,2},{1,5},{3,7},... | collective-permute-start | bytes 786440 | tf_op jit(solution)/shard_map/ppermute | solution.py:302
  9.4 1.2 %collective-permute-start.6 = (bf16[512,256]{1,0:T(8,128)(2,1)S(1)}, bf16[512,256]{1,0:T(8,128)(2,1)S(1)}, u32[]{:S(2)}, u32[]{:S(2)}) collective-permute-start(bf16[512,256]{1,0:T(8,128)(2,1)S(1)} %broadcast_select_fusion.3), channel_id=1, source_target_pairs={{0,2},{2,0},{4,6},{6,4},{8,10},{10,8},{12,14},{14,12},{1,3},{3,1},... | collective-permute-start | bytes 786440 | tf_op jit(solution)/shard_map/ppermute | solution.py:305
  10.7 5.6 %decode_pages.1.refs_0_ = bf16[288,256]{1,0:T(8,128)(2,1)S(1)} custom-call(s32[32]{0:T(128)} %refs_0_, s32[64]{0:T(128)} %refs_1_.5, bf16[64,1024]{1,0:T(8,128)(2,1)} %refs_2_.5, bf16[64,256]{1,0:T(8,128)(2,1)} %refs_3_.1, bf16[64,256]{1,0:T(8,128)(2,1)} %refs_4_.1, bf16[4096,256]{1,0:T(8,128)(2,1)} %refs_5_.1, bf16[4096,256]{1,0:T(8,128)(2,1)} %refs_6_.1), custom_call_target="tpu_custom_call" | custom-call | flops 500000000 | bytes 1048576 | tf_op jit(solution)/shard_map/decode_pages/pallas_call | solution.py:331
  16.3 0.4 collective-permute-start.4
  16.7 1.9 %collective-permute-start.2 = (bf16[512,256]{1,0:T(8,128)(2,1)S(1)}, bf16[512,256]{1,0:T(8,128)(2,1)S(1)}, u32[]{:S(2)}, u32[]{:S(2)}) collective-permute-start(bf16[512,256]{1,0:T(8,128)(2,1)S(1)} %collective-permute-done.refs_6_), channel_id=1, source_target_pairs={{0,4},{2,6},{4,8},{6,10},{8,12},{10,14},{12,0},{14,2},{1,5},{3,7},... | collective-permute-start | bytes 786440 | tf_op jit(solution)/shard_map/ppermute | solution.py:302
  18.6 1.2 %collective-permute-start.7 = (bf16[512,256]{1,0:T(8,128)(2,1)S(1)}, bf16[512,256]{1,0:T(8,128)(2,1)S(1)}, u32[]{:S(2)}, u32[]{:S(2)}) collective-permute-start(bf16[512,256]{1,0:T(8,128)(2,1)S(1)} %broadcast_select_fusion.2), channel_id=1, source_target_pairs={{0,2},{2,0},{4,6},{6,4},{8,10},{10,8},{12,14},{14,12},{1,3},{3,1},... | collective-permute-start | bytes 786440 | tf_op jit(solution)/shard_map/ppermute | solution.py:305
  20.2 0.4 collective-permute-done.4.refs_1_
  20.8 2.5 %collective-permute-done.2.refs_6_ = bf16[512,256]{1,0:T(8,128)(2,1)S(1)} collective-permute-done((bf16[512,256]{1,0:T(8,128)(2,1)S(1)}, bf16[512,256]{1,0:T(8,128)(2,1)S(1)}, u32[]{:S(2)}, u32[]{:S(2)}) %collective-permute-start.2) | collective-permute-done | bytes 262176 | tf_op jit(solution)/shard_map/ppermute | solution.py:302
  23.6 1.8 %collective-permute-start.5 = (bf16[288,256]{1,0:T(8,128)(2,1)S(1)}, bf16[288,256]{1,0:T(8,128)(2,1)S(1)}, u32[]{:S(2)}, u32[]{:S(2)}) collective-permute-start(bf16[288,256]{1,0:T(8,128)(2,1)S(1)} %decode_merge.3.refs_0_), channel_id=1, source_target_pairs={{0,4},{2,6},{4,0},{6,2},{8,12},{10,14},{12,8},{14,10},{1,5},{3,7},... | collective-permute-start | bytes 442376 | tf_op jit(solution)/shard_map/ppermute | solution.py:305
  25.4 4.1 %prompt_far.4 = (f32[2,8,256]{2,1,0:T(8,128)S(1)}, f32[2,8,256]{2,1,0:T(8,128)S(1)}, f32[2,1024,256]{2,1,0:T(8,128)S(1)}) custom-call(s32[11]{0:T(128)S(1)} %get-tuple-element.27.refs_0_, bf16[512,1024]{1,0:T(8,128)(2,1)S(1)} %copy-done, f32[2,8,256]{2,1,0:T(8,128)S(1)} %get-tuple-element.37.refs_2_, ...), custom_call_target="tpu_custom_call", output_to_operand_aliasing={{0}: (2, {}), {1}: (3, {}), {2}: (4, {})} | custom-call | flops 500000000 | bytes 1048576 | tf_op jit(solution)/shard_map/prompt_far/pallas_call | solution.py:376
  29.6 0.9 %collective-permute-start.10 = (bf16[288,256]{1,0:T(8,128)(2,1)S(1)}, bf16[288,256]{1,0:T(8,128)(2,1)S(1)}, u32[]{:S(2)}, u32[]{:S(2)}) collective-permute-start(bf16[288,256]{1,0:T(8,128)(2,1)S(1)} %decode_merge.4.refs_0_), channel_id=1, source_target_pairs={{0,8},{2,10},{4,12},{6,14},{8,0},{10,2},{12,4},{14,6},{1,9},{3,11}... | collective-permute-start | bytes 442376 | tf_op jit(solution)/shard_map/ppermute | solution.py:305
  30.4 4.1 %prompt_far.5 = (f32[2,8,256]{2,1,0:T(8,128)S(1)}, f32[2,8,256]{2,1,0:T(8,128)S(1)}, f32[2,1024,256]{2,1,0:T(8,128)S(1)}) custom-call(s32[11]{0:T(128)S(1)} %get-tuple-element.27.refs_0_, bf16[512,1024]{1,0:T(8,128)(2,1)S(1)} %copy-done, f32[2,8,256]{2,1,0:T(8,128)S(1)} %get-tuple-element.40.refs_2_, ...), custom_call_target="tpu_custom_call", output_to_operand_aliasing={{0}: (2, {}), {1}: (3, {}), {2}: (4, {})} | custom-call | flops 500000000 | bytes 1048576 | tf_op jit(solution)/shard_map/prompt_far/pallas_call | solution.py:376
  34.5 4.1 %prompt_far.6 = (f32[2,8,256]{2,1,0:T(8,128)S(1)}, f32[2,8,256]{2,1,0:T(8,128)S(1)}, f32[2,1024,256]{2,1,0:T(8,128)S(1)}) custom-call(s32[11]{0:T(128)S(1)} %get-tuple-element.27.refs_0_, bf16[512,1024]{1,0:T(8,128)(2,1)S(1)} %copy-done, f32[2,8,256]{2,1,0:T(8,128)S(1)} %get-tuple-element.43.refs_2_, ...), custom_call_target="tpu_custom_call", output_to_operand_aliasing={{0}: (2, {}), {1}: (3, {}), {2}: (4, {})} | custom-call | flops 500000000 | bytes 1048576 | tf_op jit(solution)/shard_map/prompt_far/pallas_call | solution.py:376
  38.7 4.8 %prompt_far.7 = (f32[2,8,256]{2,1,0:T(8,128)S(1)}, f32[2,8,256]{2,1,0:T(8,128)S(1)}, f32[2,1024,256]{2,1,0:T(8,128)S(1)}, bf16[512,1024]{1,0:T(8,128)(2,1)S(1)}) custom-call(s32[11]{0:T(128)S(1)} %get-tuple-element.27.refs_0_, bf16[512,1024]{1,0:T(8,128)(2,1)S(1)} %copy-done, ...), custom_call_target="tpu_custom_call", output_to_operand_aliasing={{0}: (2, {}), {1}: (3, {}), {2}: (4, {})} | custom-call | flops 500000000 | bytes 1048576 | tf_op jit(solution)/shard_map/prompt_far/pallas_call | solution.py:376
  43.6 1.4 %project_theirs.2 = bf16[288,2048]{1,0:T(8,128)(2,1)S(1)} custom-call(bf16[512,1024]{1,0:T(8,128)(2,1)S(1)} %get-tuple-element.49.refs_0_, bf16[64,1024]{1,0:T(8,128)(2,1)S(1)} %decode_merge.5.refs_1_, bf16[1024,4096]{1,0:T(8,128)(2,1)S(1)} %bitcast.2), custom_call_target="tpu_custom_call" | custom-call | flops 200000000 | bytes 1048576 | tf_op jit(solution)/shard_map/project_theirs/pallas_call | solution.py:448
  45.0 1.4 %project_theirs.3 = bf16[288,2048]{1,0:T(8,128)(2,1)S(1)} custom-call(bf16[512,1024]{1,0:T(8,128)(2,1)S(1)} %get-tuple-element.49.refs_0_, bf16[64,1024]{1,0:T(8,128)(2,1)S(1)} %decode_merge.5.refs_1_, bf16[1024,4096]{1,0:T(8,128)(2,1)S(1)} %bitcast.2), custom_call_target="tpu_custom_call" | custom-call | flops 200000000 | bytes 1048576 | tf_op jit(solution)/shard_map/project_theirs/pallas_call | solution.py:448
  46.4 5.7 %collective-permute-start.12 = (bf16[288,2048]{1,0:T(8,128)(2,1)S(1)}, bf16[288,2048]{1,0:T(8,128)(2,1)S(1)}, u32[]{:S(2)}, u32[]{:S(2)}) collective-permute-start(bf16[288,2048]{1,0:T(8,128)(2,1)S(1)} %project_theirs.3), channel_id=1, source_target_pairs={{0,1},{1,0},{2,3},{3,2},{4,5},{5,4},{6,7},{7,6},{8,9},{9,8},{10,11... | collective-permute-start | bytes 3538952 | tf_op jit(solution)/shard_map/ppermute | solution.py:461
  52.2 1.4 %project_own.3.refs_1_ = bf16[288,2048]{1,0:T(8,128)(2,1)S(1)} custom-call(bf16[512,1024]{1,0:T(8,128)(2,1)S(1)} %get-tuple-element.49.refs_0_, bf16[64,1024]{1,0:T(8,128)(2,1)S(1)} %decode_merge.5.refs_1_, bf16[1024,4096]{1,0:T(8,128)(2,1)S(1)} %bitcast.2), custom_call_target="tpu_custom_call" | custom-call | flops 200000000 | bytes 1048576 | tf_op jit(solution)/shard_map/project_own/pallas_call | solution.py:448
  53.6 1.4 %project_own.2.refs_0_ = bf16[288,2048]{1,0:T(8,128)(2,1)S(1)} custom-call(bf16[512,1024]{1,0:T(8,128)(2,1)S(1)} %get-tuple-element.49.refs_0_, bf16[64,1024]{1,0:T(8,128)(2,1)S(1)} %decode_merge.5.refs_1_, bf16[1024,4096]{1,0:T(8,128)(2,1)S(1)} %bitcast.2), custom_call_target="tpu_custom_call" | custom-call | flops 200000000 | bytes 1048576 | tf_op jit(solution)/shard_map/project_own/pallas_call | solution.py:448
  55.0 1.3 %collective-permute-done.11.refs_2_ = bf16[288,2048]{1,0:T(8,128)(2,1)S(1)} collective-permute-done((bf16[288,2048]{1,0:T(8,128)(2,1)S(1)}, bf16[288,2048]{1,0:T(8,128)(2,1)S(1)}, u32[]{:S(2)}, u32[]{:S(2)}) %collective-permute-start.11) | collective-permute-done | bytes 1179680 | tf_op jit(solution)/shard_map/ppermute | solution.py:461
  56.3 1.7 %project_finish.1 = (bf16[256,4096]{1,0:T(8,128)(2,1)}, bf16[32,4096]{1,0:T(8,128)(2,1)}) custom-call(bf16[288,2048]{1,0:T(8,128)(2,1)S(1)} %project_own.2.refs_0_, bf16[288,2048]{1,0:T(8,128)(2,1)S(1)} %project_own.3.refs_1_, bf16[288,2048]{1,0:T(8,128)(2,1)S(1)} %collective-permute-done.11.refs_2_, bf16[288,2048]{1,0:T(8,128)(2,1)S(1)} %collective-permute-done.12.refs_3_), custom_call_target="tpu_custom_call" | custom-call | flops 300000000 | bytes 1048576 | tf_op jit(solution)/shard_map/project_finish/pallas_call | solution.py:466
  (29 shorter events, 1.3 us)
Async XLA Ops:
  0.6 7.5 %collective-permute-start.1 = (bf16[512,256]{1,0:T(8,128)(2,1)}, bf16[512,256]{1,0:T(8,128)(2,1)S(1)}, u32[]{:S(2)}, u32[]{:S(2)}) collective-permute-start(bf16[512,256]{1,0:T(8,128)(2,1)} %k_ref.1), channel_id=1, source_target_pairs={{0,4},{2,6},{4,8},{6,10},{8,12},{10,14},{12,0},{14,2},{1,5},{3,7},... | collective-permute-start | bytes 786440 | tf_op jit(solution)/shard_map/ppermute | solution.py:302
  6.0 10.6 %collective-permute-start = (bf16[512,256]{1,0:T(8,128)(2,1)}, bf16[512,256]{1,0:T(8,128)(2,1)S(1)}, u32[]{:S(2)}, u32[]{:S(2)}) collective-permute-start(bf16[512,256]{1,0:T(8,128)(2,1)} %v_ref.1), channel_id=1, source_target_pairs={{0,4},{2,6},{4,8},{6,10},{8,12},{10,14},{12,0},{14,2},{1,5},{3,7},... | collective-permute-start | bytes 786440 | tf_op jit(solution)/shard_map/ppermute | solution.py:302
  8.1 11.8 %collective-permute-start.3 = (bf16[512,256]{1,0:T(8,128)(2,1)S(1)}, bf16[512,256]{1,0:T(8,128)(2,1)S(1)}, u32[]{:S(2)}, u32[]{:S(2)}) collective-permute-start(bf16[512,256]{1,0:T(8,128)(2,1)S(1)} %collective-permute-done.1.refs_5_), channel_id=1, source_target_pairs={{0,4},{2,6},{4,8},{6,10},{8,12},{10,14},{12,0},{14,2},{1,5},{3,7},... | collective-permute-start | bytes 786440 | tf_op jit(solution)/shard_map/ppermute | solution.py:302
  9.4 9.1 %copy-start.1 = (bf16[512,256]{1,0:T(8,128)(2,1)S(1)}, bf16[512,256]{1,0:T(8,128)(2,1)}, u32[]{:S(2)}) copy-start(bf16[512,256]{1,0:T(8,128)(2,1)} %v_ref.1) | copy-start | bytes 786436
  9.4 21.0 %collective-permute-start.6 = (bf16[512,256]{1,0:T(8,128)(2,1)S(1)}, bf16[512,256]{1,0:T(8,128)(2,1)S(1)}, u32[]{:S(2)}, u32[]{:S(2)}) collective-permute-start(bf16[512,256]{1,0:T(8,128)(2,1)S(1)} %broadcast_select_fusion.3), channel_id=1, source_target_pairs={{0,2},{2,0},{4,6},{6,4},{8,10},{10,8},{12,14},{14,12},{1,3},{3,1},... | collective-permute-start | bytes 786440 | tf_op jit(solution)/shard_map/ppermute | solution.py:305
  16.3 9.0 %copy-start = (bf16[512,1024]{1,0:T(8,128)(2,1)S(1)}, bf16[512,1024]{1,0:T(8,128)(2,1)}, u32[]{:S(2)}) copy-start(bf16[512,1024]{1,0:T(8,128)(2,1)} %refs_1_.9) | copy-start | bytes 3145732
  16.3 4.4 %collective-permute-start.4 = (bf16[288,256]{1,0:T(8,128)(2,1)S(1)}, bf16[288,256]{1,0:T(8,128)(2,1)S(1)}, u32[]{:S(2)}, u32[]{:S(2)}) collective-permute-start(bf16[288,256]{1,0:T(8,128)(2,1)S(1)} %decode_pages.1.refs_0_), channel_id=1, source_target_pairs={{0,2},{2,0},{4,6},{6,4},{8,10},{10,8},{12,14},{14,12},{1,3},{3,1},... | collective-permute-start | bytes 442376 | tf_op jit(solution)/shard_map/ppermute | solution.py:305
  16.7 6.6 %collective-permute-start.2 = (bf16[512,256]{1,0:T(8,128)(2,1)S(1)}, bf16[512,256]{1,0:T(8,128)(2,1)S(1)}, u32[]{:S(2)}, u32[]{:S(2)}) collective-permute-start(bf16[512,256]{1,0:T(8,128)(2,1)S(1)} %collective-permute-done.refs_6_), channel_id=1, source_target_pairs={{0,4},{2,6},{4,8},{6,10},{8,12},{10,14},{12,0},{14,2},{1,5},{3,7},... | collective-permute-start | bytes 786440 | tf_op jit(solution)/shard_map/ppermute | solution.py:302
  18.6 11.8 %collective-permute-start.7 = (bf16[512,256]{1,0:T(8,128)(2,1)S(1)}, bf16[512,256]{1,0:T(8,128)(2,1)S(1)}, u32[]{:S(2)}, u32[]{:S(2)}) collective-permute-start(bf16[512,256]{1,0:T(8,128)(2,1)S(1)} %broadcast_select_fusion.2), channel_id=1, source_target_pairs={{0,2},{2,0},{4,6},{6,4},{8,10},{10,8},{12,14},{14,12},{1,3},{3,1},... | collective-permute-start | bytes 786440 | tf_op jit(solution)/shard_map/ppermute | solution.py:305
  19.9 18.8 %collective-permute-start.8 = (bf16[512,256]{1,0:T(8,128)(2,1)S(1)}, bf16[512,256]{1,0:T(8,128)(2,1)S(1)}, u32[]{:S(2)}, u32[]{:S(2)}) collective-permute-start(bf16[512,256]{1,0:T(8,128)(2,1)S(1)} %broadcast_select_fusion.1), channel_id=1, source_target_pairs={{0,2},{2,0},{4,6},{6,4},{8,10},{10,8},{12,14},{14,12},{1,3},{3,1},... | collective-permute-start | bytes 786440 | tf_op jit(solution)/shard_map/ppermute | solution.py:305
  23.3 15.4 %collective-permute-start.9 = (bf16[512,256]{1,0:T(8,128)(2,1)S(1)}, bf16[512,256]{1,0:T(8,128)(2,1)S(1)}, u32[]{:S(2)}, u32[]{:S(2)}) collective-permute-start(bf16[512,256]{1,0:T(8,128)(2,1)S(1)} %broadcast_select_fusion), channel_id=1, source_target_pairs={{0,2},{2,0},{4,6},{6,4},{8,10},{10,8},{12,14},{14,12},{1,3},{3,1},... | collective-permute-start | bytes 786440 | tf_op jit(solution)/shard_map/ppermute | solution.py:305
  23.6 5.9 %collective-permute-start.5 = (bf16[288,256]{1,0:T(8,128)(2,1)S(1)}, bf16[288,256]{1,0:T(8,128)(2,1)S(1)}, u32[]{:S(2)}, u32[]{:S(2)}) collective-permute-start(bf16[288,256]{1,0:T(8,128)(2,1)S(1)} %decode_merge.3.refs_0_), channel_id=1, source_target_pairs={{0,4},{2,6},{4,0},{6,2},{8,12},{10,14},{12,8},{14,10},{1,5},{3,7},... | collective-permute-start | bytes 442376 | tf_op jit(solution)/shard_map/ppermute | solution.py:305
  25.4 18.3 %slice-start = ((s8[8388608]{0:T(1024)(128)(4,1)}), s8[4194304]{0:T(1024)(128)(4,1)S(1)}, s32[]{:S(2)}) async-start(s8[8388608]{0:T(1024)(128)(4,1)} %bitcast.1), calls=%async_computation | async-start | bytes 8388608
  29.6 13.9 %collective-permute-start.10 = (bf16[288,256]{1,0:T(8,128)(2,1)S(1)}, bf16[288,256]{1,0:T(8,128)(2,1)S(1)}, u32[]{:S(2)}, u32[]{:S(2)}) collective-permute-start(bf16[288,256]{1,0:T(8,128)(2,1)S(1)} %decode_merge.4.refs_0_), channel_id=1, source_target_pairs={{0,8},{2,10},{4,12},{6,14},{8,0},{10,2},{12,4},{14,6},{1,9},{3,11}... | collective-permute-start | bytes 442376 | tf_op jit(solution)/shard_map/ppermute | solution.py:305
  30.4 13.2 %slice-start.1 = ((s8[8388608]{0:T(1024)(128)(4,1)}), s8[4194304]{0:T(1024)(128)(4,1)S(1)}, s32[]{:S(2)}) async-start(s8[8388608]{0:T(1024)(128)(4,1)} %bitcast.1), calls=%async_computation.1 | async-start | bytes 8388608
  46.4 8.6 %collective-permute-start.12 = (bf16[288,2048]{1,0:T(8,128)(2,1)S(1)}, bf16[288,2048]{1,0:T(8,128)(2,1)S(1)}, u32[]{:S(2)}, u32[]{:S(2)}) collective-permute-start(bf16[288,2048]{1,0:T(8,128)(2,1)S(1)} %project_theirs.3), channel_id=1, source_target_pairs={{0,1},{1,0},{2,3},{3,2},{4,5},{5,4},{6,7},{7,6},{8,9},{9,8},{10,11... | collective-permute-start | bytes 3538952 | tf_op jit(solution)/shard_map/ppermute | solution.py:461
  52.1 4.2 %collective-permute-start.11 = (bf16[288,2048]{1,0:T(8,128)(2,1)S(1)}, bf16[288,2048]{1,0:T(8,128)(2,1)S(1)}, u32[]{:S(2)}, u32[]{:S(2)}) collective-permute-start(bf16[288,2048]{1,0:T(8,128)(2,1)S(1)} %project_theirs.2), channel_id=1, source_target_pairs={{0,1},{1,0},{2,3},{3,2},{4,5},{5,4},{6,7},{7,6},{8,9},{9,8},{10,11... | collective-permute-start | bytes 3538952 | tf_op jit(solution)/shard_map/ppermute | solution.py:461
where the time goes:
time: 58.4 us; the launch traced here: 58.2 us
  Pallas kernels  34.3 us (59%)
  starting transfers between devices  16.5 us (28%)
  waiting for transfers between devices  6.24 us (11%)
  between operations  1.02 us (2%)
    pallas_call x4, Pallas kernels, far(): pl.pallas_call(lambda *refs: far_kernel(*refs, sources=stage, last=last),...  17.1 us
    ppermute x7, starting transfers between devices, swap(): return lax.ppermute(x, 'seq', [(i, i ^ bit) for i in range(n)])  6.1 us
    ppermute x2, starting transfers between devices, on_device(): received.append(lax.ppermute(sent, 'tp', [(0, 1), (1, 0)]))  5.82 us
    pallas_call x1, Pallas kernels, decode_pages(): pl.pallas_call(lambda *refs: decode_kernel(*refs, per_request=pages * n /...  5.63 us
    pallas_call x4, Pallas kernels, project(): pl.pallas_call(lambda *refs: project_kernel(*refs, column=column, second=...  5.53 us
    ppermute x4, starting transfers between devices, ring(): return lax.ppermute(x, 'seq', [(i, (i + by) % n) for i in range(n)])  4.59 us
    ppermute x4, waiting for transfers between devices, ring(): return lax.ppermute(x, 'seq', [(i, (i + by) % n) for i in range(n)])  4.49 us
    pallas_call x1, Pallas kernels, own(): pl.pallas_call(own_kernel, in_specs=[SMEM] + [VMEM] * 4, out_specs=[SMEM]...  4.04 us
  transfers between devices with their start and end apart: 13, of which 4 were waited for; matrix products, arithmetic and copies ran while one was open for 0% of the time, Pallas kernels for 51%

commit v1 on v0

--- a/solution.py
+++ b/solution.py
@@ -30,6 +30,16 @@
     )
 
 
+def twice(k):
+    return jnp.concatenate([k, k], axis=1)
+
+
+def split_scaled(q):
+    scaled = q.astype(jnp.float32).T * SCALE2
+    high = scaled.astype(jnp.bfloat16)
+    return jnp.concatenate([high, (scaled - high.astype(jnp.float32)).astype(jnp.bfloat16)], axis=0)
+
+
 def flipped(v):
     return jnp.concatenate([v.T, jnp.ones((EXTRA, v.shape[0]), v.dtype)], axis=0)
 
@@ -46,7 +56,7 @@
     return start
 
 
-def attend_tile(q, keys, values, state, scratch, i, row_pos, docs, key_pos, win, first, diag, masked):
+def attend_tile(q_ref, keys, values, state, scratch, i, row_pos, docs, key_pos, win, first, diag, masked):
     m_ref, l_ref, acc_ref = state
     s_ref, p_ref = scratch
     heads = m_ref.shape[1]
@@ -57,7 +67,11 @@
 
     def score(h, c):
         part = slice(c, c + chunk)
-        s = scores_of(keys[h // group][part, :], q(slice(h * HD, (h + 1) * HD)))
+        s = jnp.dot(
+            keys[h // group][part, :],
+            q_ref[i, 2 * h * HD : 2 * (h + 1) * HD, :],
+            preferred_element_type=jnp.float32,
+        )
         if masked:
             if diag:
                 allowed = (key_pos[part] >= docs) & (key_pos[part] <= row_pos)
@@ -90,17 +104,17 @@
             l_ref[i, h : h + 1, :] = l_ref[i, h : h + 1, :] * shrink + pv[HD : HD + 1, :]
             acc_ref[i, columns, :] = acc_ref[i, columns, :] * shrink + pv[:HD, :]
 
-    for step in range(heads + 2):
+    for step in range(heads + 3):
         for c in range(0, span, chunk):
             if step < heads:
                 score(step, c)
             if 0 <= step - 1 < heads:
                 weigh(step - 1, c)
-            if step >= 2 and c == 0:
-                gather(step - 2)
-
-
-def own_kernel(win, doc_ref, q_ref, k_ref, v_ref, info_ref, m_ref, l_ref, acc_ref, s_ref, p_ref):
+            if step >= 3 and c == 0:
+                gather(step - 3)
+
+
+def own_kernel(win, doc_ref, q_ref, k_ref, v_ref, info_ref, m_ref, l_ref, acc_ref, q2_ref, s_ref, p_ref):
     tiles, _, tq = m_ref.shape
     kv = k_ref.shape[1] // HD
     base = lax.axis_index("seq") * (tiles * tq)
@@ -109,16 +123,19 @@
         info_ref[d] = start
     for h in range(win.shape[0]):
         info_ref[DOCS - 1 + h] = win[h]
+    for i in range(tiles):
+        for h in range(m_ref.shape[1]):
+            q = q_ref[i * tq : (i + 1) * tq, h * HD : (h + 1) * HD]
+            q2_ref[i, 2 * h * HD : 2 * (h + 1) * HD, :] = split_scaled(q)
     whole = [flipped(v_ref[:, g * HD : (g + 1) * HD]) for g in range(kv)]
     for i in range(tiles):
         span = (i + 1) * tq
         row_pos = base + i * tq + lax.broadcasted_iota(jnp.int32, (1, tq), 1)
         key_pos = base + lax.broadcasted_iota(jnp.int32, (span, tq), 0)
-        keys = [k_ref[:span, g * HD : (g + 1) * HD] for g in range(kv)]
+        keys = [twice(k_ref[:span, g * HD : (g + 1) * HD]) for g in range(kv)]
         values = [v[:, :span] for v in whole]
         attend_tile(
-            lambda columns, i=i: q_ref[i * tq : (i + 1) * tq, columns],
-            keys, values, (m_ref, l_ref, acc_ref), (s_ref, p_ref), i,
+            q2_ref, keys, values, (m_ref, l_ref, acc_ref), (s_ref, p_ref), i,
             row_pos, start_at(starts, row_pos), key_pos, win, True, True, True,
         )
 
@@ -159,13 +176,12 @@
             full = key_base >= full_low
 
             def body(masked, index=index, key_base=key_base, k_ref=k_ref, span=span):
-                keys = [k_ref[:, g * HD : (g + 1) * HD] for g in range(kv)]
+                keys = [twice(k_ref[:, g * HD : (g + 1) * HD]) for g in range(kv)]
                 values = [v_scratch[index, g] for g in range(kv)]
                 row_pos = first_row + lax.broadcasted_iota(jnp.int32, (1, tq), 1)
                 key_pos = key_base + lax.broadcasted_iota(jnp.int32, (span, tq), 0)
                 attend_tile(
-                    lambda columns: q_ref[pl.ds(pl.multiple_of(i * tq, tq), tq), columns],
-                    keys, values, (m_ref, l_ref, acc_ref), (s_ref, p_ref), i,
+                    q_ref, keys, values, (m_ref, l_ref, acc_ref), (s_ref, p_ref), i,
                     row_pos, start_at(starts, row_pos) if masked else None, key_pos, win, False, False, masked,
                 )
 
@@ -362,15 +378,19 @@
         return pl.pallas_call(
             own_kernel,
             in_specs=[SMEM] + [VMEM] * 4,
-            out_specs=[SMEM] + [VMEM] * 3,
-            out_shape=[jax.ShapeDtypeStruct((DOCS - 1 + heads,), i32)] + state,
+            out_specs=[SMEM] + [VMEM] * 4,
+            out_shape=[
+                jax.ShapeDtypeStruct((DOCS - 1 + heads,), i32),
+                *state,
+                jax.ShapeDtypeStruct((tiles, 2 * width, tq), bf16),
+            ],
             scratch_shapes=pair,
             cost_estimate=cost(3),
             compiler_params=params(16),
             name="prompt_own",
         )(*hbm(head_window, ids.reshape(-1, LANES), prefill_query, prefill_key, prefill_value))
 
-    def far(info, carry, stage, last):
+    def far(info, queries, carry, stage, last):
         operands = [x for d in stage for x in (keys[d], values[d])]
         scratch = [pltpu.VMEM((len(stage), kv, tall, tokens), bf16)] + pair
         return pl.pallas_call(
@@ -383,7 +403,7 @@
             cost_estimate=cost(5),
             compiler_params=params(20),
             name="prompt_far",
-        )(info, prefill_query, *carry, *operands)
+        )(info, queries, *carry, *operands)
 
     token = [()]
 
@@ -405,12 +425,12 @@
         table[d - 1] = swap(fresh)
 
     keys[2] = ring(prefill_key, 2)
-    info, *carry = done(*own(doc_ids))
-    values[2] = ring(then(prefill_value), 2)
+    partial = done(decode_pages(page_order))
+    other = swap(partial)
+    values[2] = ring(prefill_value, 2)
     relay(keys, 2)
-    partial = done(decode_pages(then(page_order)))
+    info, *carry, queries = done(*own(then(doc_ids)))
     relay(values, 2)
-    other = swap(partial)
     bit = 2
 
     def step(partial, other, bit):
@@ -419,22 +439,20 @@
             return partial, None, bit
         return partial, swap(partial, bit), bit * 2
 
-    def attend(d):
+    def attend(*stage):
         carry[0] = then(carry[0])
-        carry[:] = far(info, carry[:3], (d,), d == reach - 1)
+        carry[:] = far(info, queries, carry[:3], stage, stage[-1] == reach - 1)
         done(carry[0])
 
+    partial, other, bit = step(partial, other, bit)
     for d in range(4, reach + 1, 2):
         relay(keys, d)
-        if bit < n:
-            partial, other, bit = step(partial, other, bit)
+        attend(d - 2)
         relay(values, d)
-        attend(d - 2)
         if bit < n:
             partial, other, bit = step(partial, other, bit)
         attend(d - 3)
-    attend(reach)
-    attend(reach - 1)
+    attend(reach, reach - 1)
     while other is not None:
         partial, other, bit = step(partial, other, bit)
     attn, decode_attn = carry[-1], partial

time: 58.4 us -> 57.1 us (0.978)
  the two profiles are of different devices: /device:TPU:23 before, /device:TPU:25 now
where the time goes in v1:
time: 57.1 us; the launch traced here: 56.9 us
  Pallas kernels  33.3 us (58%)
  starting transfers between devices  15.2 us (27%)
  waiting for transfers between devices  7.23 us (13%)
  between operations  1.04 us (2%)
    pallas_call x3, Pallas kernels, far(): pl.pallas_call(lambda *refs: far_kernel(*refs, sources=stage, last=last),...  16 us
    ppermute x7, starting transfers between devices, swap(): return lax.ppermute(x, 'seq', [(i, i ^ bit) for i in range(n)])  6.46 us
    pallas_call x1, Pallas kernels, decode_pages(): pl.pallas_call(lambda *refs: decode_kernel(*refs, per_request=pages * n /...  5.68 us
    pallas_call x4, Pallas kernels, project(): pl.pallas_call(lambda *refs: project_kernel(*refs, column=column, second=...  5.53 us
    ppermute x2, starting transfers between devices, on_device(): received.append(lax.ppermute(sent, 'tp', [(0, 1), (1, 0)]))  4.54 us
    ppermute x4, starting transfers between devices, ring(): return lax.ppermute(x, 'seq', [(i, (i + by) % n) for i in range(n)])  4.24 us
    pallas_call x1, Pallas kernels, own(): pl.pallas_call(own_kernel, in_specs=[SMEM] + [VMEM] * 4, out_specs=[SMEM]...  4.06 us
    ppermute x4, waiting for transfers between devices, ring(): return lax.ppermute(x, 'seq', [(i, (i + by) % n) for i in range(n)])  3.24 us
  transfers between devices with their start and end apart: 13, of which 4 were waited for; matrix products, arithmetic and copies ran while one was open for 0% of the time, Pallas kernels for 37%

profile of v1, /device:TPU:25, one launch (start us, length us, event | category | flops | bytes accessed | tf_op | source)
XLA Modules:
  0.0 56.9 jit_solution(17502833161388021050)
XLA Ops:
  0.7 5.7 %decode_pages.1.refs_0_ = bf16[288,256]{1,0:T(8,128)(2,1)S(1)} custom-call(s32[32]{0:T(128)} %refs_0_.1, s32[64]{0:T(128)} %refs_1_.1, bf16[64,1024]{1,0:T(8,128)(2,1)} %refs_2_.5, bf16[64,256]{1,0:T(8,128)(2,1)} %refs_3_.1, bf16[64,256]{1,0:T(8,128)(2,1)} %refs_4_.1, bf16[4096,256]{1,0:T(8,128)(2,1)} %refs_5_.1, bf16[4096,256]{1,0:T(8,128)(2,1)} %refs_6_.1), custom_call_target="tpu_custom_call" | custom-call | flops 500000000 | bytes 1048576 | tf_op jit(solution)/shard_map/decode_pages/pallas_call | solution.py:347
  6.4 1.3 %collective-permute-start.3 = (bf16[288,256]{1,0:T(8,128)(2,1)S(1)}, bf16[288,256]{1,0:T(8,128)(2,1)S(1)}, u32[]{:S(2)}, u32[]{:S(2)}) collective-permute-start(bf16[288,256]{1,0:T(8,128)(2,1)S(1)} %decode_pages.1.refs_0_), channel_id=1, source_target_pairs={{0,2},{2,0},{4,6},{6,4},{8,10},{10,8},{12,14},{14,12},{1,3},{3,1},... | collective-permute-start | bytes 442376 | tf_op jit(solution)/shard_map/ppermute | solution.py:321
  7.7 1.2 %collective-permute-start.2 = (bf16[512,256]{1,0:T(8,128)(2,1)S(1)}, bf16[512,256]{1,0:T(8,128)(2,1)S(1)}, u32[]{:S(2)}, u32[]{:S(2)}) collective-permute-start(bf16[512,256]{1,0:T(8,128)(2,1)S(1)} %copy-done.1), channel_id=1, source_target_pairs={{0,4},{2,6},{4,8},{6,10},{8,12},{10,14},{12,0},{14,2},{1,5},{3,7},... | collective-permute-start | bytes 786440 | tf_op jit(solution)/shard_map/ppermute | solution.py:318
  8.9 1.3 %collective-permute-start.1 = (bf16[512,256]{1,0:T(8,128)(2,1)S(1)}, bf16[512,256]{1,0:T(8,128)(2,1)S(1)}, u32[]{:S(2)}, u32[]{:S(2)}) collective-permute-start(bf16[512,256]{1,0:T(8,128)(2,1)S(1)} %collective-permute-done.refs_5_), channel_id=1, source_target_pairs={{0,4},{2,6},{4,8},{6,10},{8,12},{10,14},{12,0},{14,2},{1,5},{3,7},... | collective-permute-start | bytes 786440 | tf_op jit(solution)/shard_map/ppermute | solution.py:318
  10.2 1.1 %collective-permute-start.6 = (bf16[512,256]{1,0:T(8,128)(2,1)S(1)}, bf16[512,256]{1,0:T(8,128)(2,1)S(1)}, u32[]{:S(2)}, u32[]{:S(2)}) collective-permute-start(bf16[512,256]{1,0:T(8,128)(2,1)S(1)} %broadcast_select_fusion.3), channel_id=1, source_target_pairs={{0,2},{2,0},{4,6},{6,4},{8,10},{10,8},{12,14},{14,12},{1,3},{3,1},... | collective-permute-start | bytes 786440 | tf_op jit(solution)/shard_map/ppermute | solution.py:321
  11.3 4.1 %prompt_own.1 = (s32[11]{0:T(128)S(1)}, f32[2,8,256]{2,1,0:T(8,128)S(1)}, f32[2,8,256]{2,1,0:T(8,128)S(1)}, f32[2,1024,256]{2,1,0:T(8,128)S(1)}, bf16[2,2048,256]{2,1,0:T(8,128)(2,1)S(1)}) custom-call(s32[8]{0:T(128)} %win.1, s32[32,128]{1,0:T(8,128)} %bitcast.3, bf16[512,1024]{1,0:T(8,128)(2,1)} %q_ref.1, bf16[512,256]{1,0:T(8,128)(2,1)} %k_ref.1, ...), custom_call_target="tpu_custom_call" | custom-call | flops 300000000 | bytes 1048576 | tf_op jit(solution)/shard_map/prompt_own/pallas_call | solution.py:378
  15.4 0.5 collective-permute-start.7
  16.0 1.7 %collective-permute-start.4 = (bf16[512,256]{1,0:T(8,128)(2,1)S(1)}, bf16[512,256]{1,0:T(8,128)(2,1)S(1)}, u32[]{:S(2)}, u32[]{:S(2)}) collective-permute-start(bf16[512,256]{1,0:T(8,128)(2,1)S(1)} %collective-permute-done.2.refs_6_), channel_id=1, source_target_pairs={{0,4},{2,6},{4,8},{6,10},{8,12},{10,14},{12,0},{14,2},{1,5},{3,7},... | collective-permute-start | bytes 786440 | tf_op jit(solution)/shard_map/ppermute | solution.py:318
  17.8 2.3 %collective-permute-done.1.refs_5_ = bf16[512,256]{1,0:T(8,128)(2,1)S(1)} collective-permute-done((bf16[512,256]{1,0:T(8,128)(2,1)S(1)}, bf16[512,256]{1,0:T(8,128)(2,1)S(1)}, u32[]{:S(2)}, u32[]{:S(2)}) %collective-permute-start.1) | collective-permute-done | bytes 262176 | tf_op jit(solution)/shard_map/ppermute | solution.py:318
  20.1 0.4 collective-permute-start.8
  20.6 4.2 %prompt_far.3 = (f32[2,8,256]{2,1,0:T(8,128)S(1)}, f32[2,8,256]{2,1,0:T(8,128)S(1)}, f32[2,1024,256]{2,1,0:T(8,128)S(1)}) custom-call(s32[11]{0:T(128)S(1)} %get-tuple-element.27.refs_0_, bf16[2,2048,256]{2,1,0:T(8,128)(2,1)S(1)} %get-tuple-element.28.refs_1_, ...), custom_call_target="tpu_custom_call", output_to_operand_aliasing={{0}: (2, {}), {1}: (3, {}), {2}: (4, {})} | custom-call | flops 500000000 | bytes 1048576 | tf_op jit(solution)/shard_map/prompt_far/pallas_call | solution.py:396
  24.8 1.0 %collective-permute-done.4.refs_6_ = bf16[512,256]{1,0:T(8,128)(2,1)S(1)} collective-permute-done((bf16[512,256]{1,0:T(8,128)(2,1)S(1)}, bf16[512,256]{1,0:T(8,128)(2,1)S(1)}, u32[]{:S(2)}, u32[]{:S(2)}) %collective-permute-start.4) | collective-permute-done | bytes 262176 | tf_op jit(solution)/shard_map/ppermute | solution.py:318
  25.7 0.4 collective-permute-start.9
  26.2 2.7 %collective-permute-done.5.refs_1_ = bf16[288,256]{1,0:T(8,128)(2,1)S(1)} collective-permute-done((bf16[288,256]{1,0:T(8,128)(2,1)S(1)}, bf16[288,256]{1,0:T(8,128)(2,1)S(1)}, u32[]{:S(2)}, u32[]{:S(2)}) %collective-permute-start.5) | collective-permute-done | bytes 147488 | tf_op jit(solution)/shard_map/ppermute | solution.py:321
  29.0 2.6 %collective-permute-start.10 = (bf16[288,256]{1,0:T(8,128)(2,1)S(1)}, bf16[288,256]{1,0:T(8,128)(2,1)S(1)}, u32[]{:S(2)}, u32[]{:S(2)}) collective-permute-start(bf16[288,256]{1,0:T(8,128)(2,1)S(1)} %decode_merge.4.refs_0_), channel_id=1, source_target_pairs={{0,8},{2,10},{4,12},{6,14},{8,0},{10,2},{12,4},{14,6},{1,9},{3,11}... | collective-permute-start | bytes 442376 | tf_op jit(solution)/shard_map/ppermute | solution.py:321
  31.6 3.9 %prompt_far.4 = (f32[2,8,256]{2,1,0:T(8,128)S(1)}, f32[2,8,256]{2,1,0:T(8,128)S(1)}, f32[2,1024,256]{2,1,0:T(8,128)S(1)}) custom-call(s32[11]{0:T(128)S(1)} %get-tuple-element.27.refs_0_, bf16[2,2048,256]{2,1,0:T(8,128)(2,1)S(1)} %get-tuple-element.28.refs_1_, ...), custom_call_target="tpu_custom_call", output_to_operand_aliasing={{0}: (2, {}), {1}: (3, {}), {2}: (4, {})} | custom-call | flops 500000000 | bytes 1048576 | tf_op jit(solution)/shard_map/prompt_far/pallas_call | solution.py:396
  35.6 8.0 %prompt_far.5 = (f32[2,8,256]{2,1,0:T(8,128)S(1)}, f32[2,8,256]{2,1,0:T(8,128)S(1)}, f32[2,1024,256]{2,1,0:T(8,128)S(1)}, bf16[512,1024]{1,0:T(8,128)(2,1)S(1)}) custom-call(s32[11]{0:T(128)S(1)} %get-tuple-element.27.refs_0_, bf16[2,2048,256]{2,1,0:T(8,128)(2,1)S(1)} %get-tuple-element.28.refs_1_, ...), custom_call_target="tpu_custom_call", output_to_operand_aliasing={{0}: (2, {}), {1}: (3, {}), {2}: (4, {})} | custom-call | flops 500000000 | bytes 1048576 | tf_op jit(solution)/shard_map/prompt_far/pallas_call | solution.py:396
  43.6 1.4 %project_theirs.2 = bf16[288,2048]{1,0:T(8,128)(2,1)S(1)} custom-call(bf16[512,1024]{1,0:T(8,128)(2,1)S(1)} %get-tuple-element.45.refs_0_, bf16[64,1024]{1,0:T(8,128)(2,1)S(1)} %decode_merge.5.refs_1_, bf16[1024,4096]{1,0:T(8,128)(2,1)S(1)} %bitcast.2), custom_call_target="tpu_custom_call" | custom-call | flops 200000000 | bytes 1048576 | tf_op jit(solution)/shard_map/project_theirs/pallas_call | solution.py:466
  45.0 1.4 %project_theirs.3 = bf16[288,2048]{1,0:T(8,128)(2,1)S(1)} custom-call(bf16[512,1024]{1,0:T(8,128)(2,1)S(1)} %get-tuple-element.45.refs_0_, bf16[64,1024]{1,0:T(8,128)(2,1)S(1)} %decode_merge.5.refs_1_, bf16[1024,4096]{1,0:T(8,128)(2,1)S(1)} %bitcast.2), custom_call_target="tpu_custom_call" | custom-call | flops 200000000 | bytes 1048576 | tf_op jit(solution)/shard_map/project_theirs/pallas_call | solution.py:466
  46.4 4.5 %collective-permute-start.12 = (bf16[288,2048]{1,0:T(8,128)(2,1)S(1)}, bf16[288,2048]{1,0:T(8,128)(2,1)S(1)}, u32[]{:S(2)}, u32[]{:S(2)}) collective-permute-start(bf16[288,2048]{1,0:T(8,128)(2,1)S(1)} %project_theirs.3), channel_id=1, source_target_pairs={{0,1},{1,0},{2,3},{3,2},{4,5},{5,4},{6,7},{7,6},{8,9},{9,8},{10,11... | collective-permute-start | bytes 3538952 | tf_op jit(solution)/shard_map/ppermute | solution.py:479
  51.0 1.4 %project_own.3.refs_1_ = bf16[288,2048]{1,0:T(8,128)(2,1)S(1)} custom-call(bf16[512,1024]{1,0:T(8,128)(2,1)S(1)} %get-tuple-element.45.refs_0_, bf16[64,1024]{1,0:T(8,128)(2,1)S(1)} %decode_merge.5.refs_1_, bf16[1024,4096]{1,0:T(8,128)(2,1)S(1)} %bitcast.2), custom_call_target="tpu_custom_call" | custom-call | flops 200000000 | bytes 1048576 | tf_op jit(solution)/shard_map/project_own/pallas_call | solution.py:466
  52.3 1.4 %project_own.2.refs_0_ = bf16[288,2048]{1,0:T(8,128)(2,1)S(1)} custom-call(bf16[512,1024]{1,0:T(8,128)(2,1)S(1)} %get-tuple-element.45.refs_0_, bf16[64,1024]{1,0:T(8,128)(2,1)S(1)} %decode_merge.5.refs_1_, bf16[1024,4096]{1,0:T(8,128)(2,1)S(1)} %bitcast.2), custom_call_target="tpu_custom_call" | custom-call | flops 200000000 | bytes 1048576 | tf_op jit(solution)/shard_map/project_own/pallas_call | solution.py:466
  53.7 1.3 %collective-permute-done.11.refs_2_ = bf16[288,2048]{1,0:T(8,128)(2,1)S(1)} collective-permute-done((bf16[288,2048]{1,0:T(8,128)(2,1)S(1)}, bf16[288,2048]{1,0:T(8,128)(2,1)S(1)}, u32[]{:S(2)}, u32[]{:S(2)}) %collective-permute-start.11) | collective-permute-done | bytes 1179680 | tf_op jit(solution)/shard_map/ppermute | solution.py:479
  55.0 1.7 %project_finish.1 = (bf16[256,4096]{1,0:T(8,128)(2,1)}, bf16[32,4096]{1,0:T(8,128)(2,1)}) custom-call(bf16[288,2048]{1,0:T(8,128)(2,1)S(1)} %project_own.2.refs_0_, bf16[288,2048]{1,0:T(8,128)(2,1)S(1)} %project_own.3.refs_1_, bf16[288,2048]{1,0:T(8,128)(2,1)S(1)} %collective-permute-done.11.refs_2_, bf16[288,2048]{1,0:T(8,128)(2,1)S(1)} %collective-permute-done.12.refs_3_), custom_call_target="tpu_custom_call" | custom-call | flops 300000000 | bytes 1048576 | tf_op jit(solution)/shard_map/project_finish/pallas_call | solution.py:484
  (30 shorter events, 0.7 us)
Async XLA Ops:
  0.6 9.6 %copy-start = (bf16[512,256]{1,0:T(8,128)(2,1)S(1)}, bf16[512,256]{1,0:T(8,128)(2,1)}, u32[]{:S(2)}) copy-start(bf16[512,256]{1,0:T(8,128)(2,1)} %k_ref.1) | copy-start | bytes 786436
  0.6 7.1 %copy-start.1 = (bf16[512,256]{1,0:T(8,128)(2,1)S(1)}, bf16[512,256]{1,0:T(8,128)(2,1)}, u32[]{:S(2)}) copy-start(bf16[512,256]{1,0:T(8,128)(2,1)} %v_ref.1) | copy-start | bytes 786436
  0.7 8.2 %collective-permute-start = (bf16[512,256]{1,0:T(8,128)(2,1)}, bf16[512,256]{1,0:T(8,128)(2,1)S(1)}, u32[]{:S(2)}, u32[]{:S(2)}) collective-permute-start(bf16[512,256]{1,0:T(8,128)(2,1)} %k_ref.1), channel_id=1, source_target_pairs={{0,4},{2,6},{4,8},{6,10},{8,12},{10,14},{12,0},{14,2},{1,5},{3,7},... | collective-permute-start | bytes 786440 | tf_op jit(solution)/shard_map/ppermute | solution.py:318
  6.4 9.0 %copy-start.2 = (bf16[512,256]{1,0:T(8,128)(2,1)S(1)}, bf16[512,256]{1,0:T(8,128)(2,1)}, u32[]{:S(2)}) copy-start(bf16[512,256]{1,0:T(8,128)(2,1)} %v_ref.1) | copy-start | bytes 786436
  6.4 11.2 %collective-permute-start.3 = (bf16[288,256]{1,0:T(8,128)(2,1)S(1)}, bf16[288,256]{1,0:T(8,128)(2,1)S(1)}, u32[]{:S(2)}, u32[]{:S(2)}) collective-permute-start(bf16[288,256]{1,0:T(8,128)(2,1)S(1)} %decode_pages.1.refs_0_), channel_id=1, source_target_pairs={{0,2},{2,0},{4,6},{6,4},{8,10},{10,8},{12,14},{14,12},{1,3},{3,1},... | collective-permute-start | bytes 442376 | tf_op jit(solution)/shard_map/ppermute | solution.py:321
  7.7 7.7 %collective-permute-start.2 = (bf16[512,256]{1,0:T(8,128)(2,1)S(1)}, bf16[512,256]{1,0:T(8,128)(2,1)S(1)}, u32[]{:S(2)}, u32[]{:S(2)}) collective-permute-start(bf16[512,256]{1,0:T(8,128)(2,1)S(1)} %copy-done.1), channel_id=1, source_target_pairs={{0,4},{2,6},{4,8},{6,10},{8,12},{10,14},{12,0},{14,2},{1,5},{3,7},... | collective-permute-start | bytes 786440 | tf_op jit(solution)/shard_map/ppermute | solution.py:318
  8.9 11.2 %collective-permute-start.1 = (bf16[512,256]{1,0:T(8,128)(2,1)S(1)}, bf16[512,256]{1,0:T(8,128)(2,1)S(1)}, u32[]{:S(2)}, u32[]{:S(2)}) collective-permute-start(bf16[512,256]{1,0:T(8,128)(2,1)S(1)} %collective-permute-done.refs_5_), channel_id=1, source_target_pairs={{0,4},{2,6},{4,8},{6,10},{8,12},{10,14},{12,0},{14,2},{1,5},{3,7},... | collective-permute-start | bytes 786440 | tf_op jit(solution)/shard_map/ppermute | solution.py:318
  10.2 21.3 %collective-permute-start.6 = (bf16[512,256]{1,0:T(8,128)(2,1)S(1)}, bf16[512,256]{1,0:T(8,128)(2,1)S(1)}, u32[]{:S(2)}, u32[]{:S(2)}) collective-permute-start(bf16[512,256]{1,0:T(8,128)(2,1)S(1)} %broadcast_select_fusion.3), channel_id=1, source_target_pairs={{0,2},{2,0},{4,6},{6,4},{8,10},{10,8},{12,14},{14,12},{1,3},{3,1},... | collective-permute-start | bytes 786440 | tf_op jit(solution)/shard_map/ppermute | solution.py:321
  15.4 16.1 %collective-permute-start.7 = (bf16[512,256]{1,0:T(8,128)(2,1)S(1)}, bf16[512,256]{1,0:T(8,128)(2,1)S(1)}, u32[]{:S(2)}, u32[]{:S(2)}) collective-permute-start(bf16[512,256]{1,0:T(8,128)(2,1)S(1)} %broadcast_select_fusion.2), channel_id=1, source_target_pairs={{0,2},{2,0},{4,6},{6,4},{8,10},{10,8},{12,14},{14,12},{1,3},{3,1},... | collective-permute-start | bytes 786440 | tf_op jit(solution)/shard_map/ppermute | solution.py:321
  16.0 9.8 %collective-permute-start.4 = (bf16[512,256]{1,0:T(8,128)(2,1)S(1)}, bf16[512,256]{1,0:T(8,128)(2,1)S(1)}, u32[]{:S(2)}, u32[]{:S(2)}) collective-permute-start(bf16[512,256]{1,0:T(8,128)(2,1)S(1)} %collective-permute-done.2.refs_6_), channel_id=1, source_target_pairs={{0,4},{2,6},{4,8},{6,10},{8,12},{10,14},{12,0},{14,2},{1,5},{3,7},... | collective-permute-start | bytes 786440 | tf_op jit(solution)/shard_map/ppermute | solution.py:318
  17.7 11.1 %collective-permute-start.5 = (bf16[288,256]{1,0:T(8,128)(2,1)S(1)}, bf16[288,256]{1,0:T(8,128)(2,1)S(1)}, u32[]{:S(2)}, u32[]{:S(2)}) collective-permute-start(bf16[288,256]{1,0:T(8,128)(2,1)S(1)} %decode_merge.3.refs_0_), channel_id=1, source_target_pairs={{0,4},{2,6},{4,0},{6,2},{8,12},{10,14},{12,8},{14,10},{1,5},{3,7},... | collective-permute-start | bytes 442376 | tf_op jit(solution)/shard_map/ppermute | solution.py:321
  20.1 15.5 %collective-permute-start.8 = (bf16[512,256]{1,0:T(8,128)(2,1)S(1)}, bf16[512,256]{1,0:T(8,128)(2,1)S(1)}, u32[]{:S(2)}, u32[]{:S(2)}) collective-permute-start(bf16[512,256]{1,0:T(8,128)(2,1)S(1)} %broadcast_select_fusion.1), channel_id=1, source_target_pairs={{0,2},{2,0},{4,6},{6,4},{8,10},{10,8},{12,14},{14,12},{1,3},{3,1},... | collective-permute-start | bytes 786440 | tf_op jit(solution)/shard_map/ppermute | solution.py:321
  20.6 23.0 %slice-start = ((s8[8388608]{0:T(1024)(128)(4,1)}), s8[4194304]{0:T(1024)(128)(4,1)S(1)}, s32[]{:S(2)}) async-start(s8[8388608]{0:T(1024)(128)(4,1)} %bitcast.1), calls=%async_computation | async-start | bytes 8388608
  25.7 9.9 %collective-permute-start.9 = (bf16[512,256]{1,0:T(8,128)(2,1)S(1)}, bf16[512,256]{1,0:T(8,128)(2,1)S(1)}, u32[]{:S(2)}, u32[]{:S(2)}) collective-permute-start(bf16[512,256]{1,0:T(8,128)(2,1)S(1)} %broadcast_select_fusion), channel_id=1, source_target_pairs={{0,2},{2,0},{4,6},{6,4},{8,10},{10,8},{12,14},{14,12},{1,3},{3,1},... | collective-permute-start | bytes 786440 | tf_op jit(solution)/shard_map/ppermute | solution.py:321
  29.0 6.5 %collective-permute-start.10 = (bf16[288,256]{1,0:T(8,128)(2,1)S(1)}, bf16[288,256]{1,0:T(8,128)(2,1)S(1)}, u32[]{:S(2)}, u32[]{:S(2)}) collective-permute-start(bf16[288,256]{1,0:T(8,128)(2,1)S(1)} %decode_merge.4.refs_0_), channel_id=1, source_target_pairs={{0,8},{2,10},{4,12},{6,14},{8,0},{10,2},{12,4},{14,6},{1,9},{3,11}... | collective-permute-start | bytes 442376 | tf_op jit(solution)/shard_map/ppermute | solution.py:321
  31.6 12.1 %slice-start.1 = ((s8[8388608]{0:T(1024)(128)(4,1)}), s8[4194304]{0:T(1024)(128)(4,1)S(1)}, s32[]{:S(2)}) async-start(s8[8388608]{0:T(1024)(128)(4,1)} %bitcast.1), calls=%async_computation.1 | async-start | bytes 8388608
  46.4 7.3 %collective-permute-start.12 = (bf16[288,2048]{1,0:T(8,128)(2,1)S(1)}, bf16[288,2048]{1,0:T(8,128)(2,1)S(1)}, u32[]{:S(2)}, u32[]{:S(2)}) collective-permute-start(bf16[288,2048]{1,0:T(8,128)(2,1)S(1)} %project_theirs.3), channel_id=1, source_target_pairs={{0,1},{1,0},{2,3},{3,2},{4,5},{5,4},{6,7},{7,6},{8,9},{9,8},{10,11... | collective-permute-start | bytes 3538952 | tf_op jit(solution)/shard_map/ppermute | solution.py:479
  50.9 4.2 %collective-permute-start.11 = (bf16[288,2048]{1,0:T(8,128)(2,1)S(1)}, bf16[288,2048]{1,0:T(8,128)(2,1)S(1)}, u32[]{:S(2)}, u32[]{:S(2)}) collective-permute-start(bf16[288,2048]{1,0:T(8,128)(2,1)S(1)} %project_theirs.2), channel_id=1, source_target_pairs={{0,1},{1,0},{2,3},{3,2},{4,5},{5,4},{6,7},{7,6},{8,9},{9,8},{10,11... | collective-permute-start | bytes 3538952 | tf_op jit(solution)/shard_map/ppermute | solution.py:479

commit v2 on v1

--- a/solution.py
+++ b/solution.py
@@ -283,21 +283,31 @@
     )
 
 
-def finish_kernel(*refs):
-    po_ref, do_ref, s_ref, sems = refs[-4:]
-    count = (len(refs) - 4) // 2
-    tr = po_ref.shape[0]
-    cols = refs[0].shape[1]
+def emit(mine, other, s_ref, sems, outs, column):
+    po_ref, do_ref = outs
+    tr, cols = po_ref.shape[0], s_ref.shape[1]
+    size = cols // 2
     copies = []
-    for c in range(count):
-        part = slice(c * cols, (c + 1) * cols)
-        total = refs[c][...].astype(jnp.float32) + refs[count + c][...].astype(jnp.float32)
-        s_ref[:, part] = total.astype(jnp.bfloat16)
-        copies.append(pltpu.make_async_copy(s_ref.at[:tr, part], po_ref.at[:, part], sems.at[2 * c]))
-        copies.append(pltpu.make_async_copy(s_ref.at[tr:, part], do_ref.at[:, part], sems.at[2 * c + 1]))
+    for c in range(2):
+        here, there = pl.ds(c * size, size), pl.ds(column + c * size, size)
+        total = mine[:, here].astype(jnp.float32) + other[:, here].astype(jnp.float32)
+        s_ref[:, here] = total.astype(jnp.bfloat16)
+        copies.append(pltpu.make_async_copy(s_ref.at[:tr, here], po_ref.at[:, there], sems.at[2 * c]))
+        copies.append(pltpu.make_async_copy(s_ref.at[tr:, here], do_ref.at[:, there], sems.at[2 * c + 1]))
         copies[-2].start()
         copies[-1].start()
+    return copies
+
+
+def early_kernel(a_ref, d_ref, w_ref, mine_ref, r_ref, po_ref, do_ref, next_ref, s_ref, sems):
+    copies = emit(mine_ref, r_ref, s_ref, sems, (po_ref, do_ref), 0)
+    project_kernel(a_ref, d_ref, w_ref, next_ref, column=mine_ref.shape[1], second=1)
     for copy in copies:
+        copy.wait()
+
+
+def late_kernel(mine_ref, r_ref, _po, _do, po_ref, do_ref, s_ref, sems):
+    for copy in emit(mine_ref, r_ref, s_ref, sems, (po_ref, do_ref), mine_ref.shape[1]):
         copy.wait()
 
 
@@ -473,24 +483,37 @@
             name="project_own" if second else "project_theirs",
         )(attn, decode_attn, out_proj)
 
-    mine, received = [], []
+    received = []
     for c in range(chunks):
         sent = project(c * cols, 0)
         received.append(lax.ppermute(sent, "tp", [(0, 1), (1, 0)]))
         decode_attn = lax.optimization_barrier((decode_attn, sent))[0]
-    for c in range(chunks):
-        mine.append(project(c * cols, 1))
+    outs = [jax.ShapeDtypeStruct((tr, model), bf16), jax.ShapeDtypeStruct((dr, model), bf16)]
+    anywhere = [pl.BlockSpec(memory_space=pl.ANY)] * 2
+    buffers = [pltpu.VMEM((tr + dr, cols), bf16), pltpu.SemaphoreType.DMA((4,))]
+    mine = project(0, 1)
+    *outputs, mine = pl.pallas_call(
+        early_kernel,
+        in_specs=[VMEM] * 5,
+        out_specs=anywhere + [VMEM],
+        out_shape=outs + [jax.ShapeDtypeStruct((tr + dr, cols), bf16)],
+        scratch_shapes=buffers,
+        cost_estimate=cost(2),
+        compiler_params=params(16),
+        name="project_early",
+    )(attn, decode_attn, out_proj, mine, received[0])
     return tuple(
         pl.pallas_call(
-            finish_kernel,
-            in_specs=[VMEM] * (2 * chunks),
-            out_specs=[pl.BlockSpec(memory_space=pl.ANY)] * 2,
-            out_shape=[jax.ShapeDtypeStruct((tr, model), bf16), jax.ShapeDtypeStruct((dr, model), bf16)],
-            scratch_shapes=[pltpu.VMEM((tr + dr, model), bf16), pltpu.SemaphoreType.DMA((2 * chunks,))],
-            cost_estimate=cost(3),
-            compiler_params=params(12),
-            name="project_finish",
-        )(*mine, *received)
+            late_kernel,
+            in_specs=[VMEM] * 2 + anywhere,
+            out_specs=anywhere,
+            out_shape=outs,
+            input_output_aliases={2: 0, 3: 1},
+            scratch_shapes=buffers,
+            cost_estimate=cost(1),
+            compiler_params=params(8),
+            name="project_late",
+        )(mine, received[1], *outputs)
     )
 
 

time: 57.1 us -> 56.8 us (level)
  waiting for transfers between devices: 7.23 us -> 5.86 us
  Pallas kernels: 33.3 us -> 34.4 us
    pallas_call x1 -> x2, Pallas kernels: 1.73 us -> 3.92 us  [the longest x1 2.75 us: on_device(): pl.pallas_call(early_kernel, in_specs=[VMEM] * 5, out_specs=anywhere + [V...]
    pallas_call x4 -> x3, Pallas kernels: 5.53 us -> 4.15 us  [project(): pl.pallas_call(lambda *refs: project_kernel(*refs, column=column, second=...]
    ppermute x2, waiting for transfers between devices: 1.29 us -> 0.01 us  [on_device(): received.append(lax.ppermute(sent, 'tp', [(0, 1), (1, 0)]))]
  transfers between devices with their start and end apart: 13 -> 13, of which waited for: 4 -> 3; matrix products, arithmetic and copies ran while one was open for 0% -> 0% of each run, Pallas kernels for 37% -> 42%
where the time goes in v2:
time: 56.8 us; the launch traced here: 56.6 us
  Pallas kernels  34.4 us (61%)
  starting transfers between devices  15.2 us (27%)
  waiting for transfers between devices  5.86 us (10%)
  between operations  1.05 us (2%)
    pallas_call x3, Pallas kernels, far(): pl.pallas_call(lambda *refs: far_kernel(*refs, sources=stage, last=last),...  16.3 us
    ppermute x7, starting transfers between devices, swap(): return lax.ppermute(x, 'seq', [(i, i ^ bit) for i in range(n)])  6.47 us
    pallas_call x1, Pallas kernels, decode_pages(): pl.pallas_call(lambda *refs: decode_kernel(*refs, per_request=pages * n /...  5.68 us
    ppermute x2, starting transfers between devices, on_device(): received.append(lax.ppermute(sent, 'tp', [(0, 1), (1, 0)]))  4.47 us
    ppermute x4, starting transfers between devices, ring(): return lax.ppermute(x, 'seq', [(i, (i + by) % n) for i in range(n)])  4.21 us
    pallas_call x3, Pallas kernels, project(): pl.pallas_call(lambda *refs: project_kernel(*refs, column=column, second=...  4.15 us
    pallas_call x1, Pallas kernels, own(): pl.pallas_call(own_kernel, in_specs=[SMEM] + [VMEM] * 4, out_specs=[SMEM]...  4.07 us
    ppermute x4, waiting for transfers between devices, ring(): return lax.ppermute(x, 'seq', [(i, (i + by) % n) for i in range(n)])  3.16 us
  transfers between devices with their start and end apart: 13, of which 3 were waited for; matrix products, arithmetic and copies ran while one was open for 0% of the time, Pallas kernels for 42%

profile of v2, /device:TPU:25, one launch (start us, length us, event | category | flops | bytes accessed | tf_op | source)
XLA Modules:
  0.0 56.6 jit_solution(6573065719175715074)
XLA Ops:
  0.7 5.7 %decode_pages.1.refs_0_ = bf16[288,256]{1,0:T(8,128)(2,1)S(1)} custom-call(s32[32]{0:T(128)} %refs_0_.1, s32[64]{0:T(128)} %refs_1_.1, bf16[64,1024]{1,0:T(8,128)(2,1)} %refs_2_.4, bf16[64,256]{1,0:T(8,128)(2,1)} %refs_3_.1, bf16[64,256]{1,0:T(8,128)(2,1)} %refs_4_.1, bf16[4096,256]{1,0:T(8,128)(2,1)} %refs_5_.1, bf16[4096,256]{1,0:T(8,128)(2,1)} %refs_6_.1), custom_call_target="tpu_custom_call" | custom-call | flops 500000000 | bytes 1048576 | tf_op jit(solution)/shard_map/decode_pages/pallas_call | solution.py:357
  6.4 1.3 %collective-permute-start.3 = (bf16[288,256]{1,0:T(8,128)(2,1)S(1)}, bf16[288,256]{1,0:T(8,128)(2,1)S(1)}, u32[]{:S(2)}, u32[]{:S(2)}) collective-permute-start(bf16[288,256]{1,0:T(8,128)(2,1)S(1)} %decode_pages.1.refs_0_), channel_id=1, source_target_pairs={{0,2},{2,0},{4,6},{6,4},{8,10},{10,8},{12,14},{14,12},{1,3},{3,1},... | collective-permute-start | bytes 442376 | tf_op jit(solution)/shard_map/ppermute | solution.py:331
  7.7 1.2 %collective-permute-start.2 = (bf16[512,256]{1,0:T(8,128)(2,1)S(1)}, bf16[512,256]{1,0:T(8,128)(2,1)S(1)}, u32[]{:S(2)}, u32[]{:S(2)}) collective-permute-start(bf16[512,256]{1,0:T(8,128)(2,1)S(1)} %copy-done.1), channel_id=1, source_target_pairs={{0,4},{2,6},{4,8},{6,10},{8,12},{10,14},{12,0},{14,2},{1,5},{3,7},... | collective-permute-start | bytes 786440 | tf_op jit(solution)/shard_map/ppermute | solution.py:328
  8.9 1.3 %collective-permute-start.1 = (bf16[512,256]{1,0:T(8,128)(2,1)S(1)}, bf16[512,256]{1,0:T(8,128)(2,1)S(1)}, u32[]{:S(2)}, u32[]{:S(2)}) collective-permute-start(bf16[512,256]{1,0:T(8,128)(2,1)S(1)} %collective-permute-done.refs_5_), channel_id=1, source_target_pairs={{0,4},{2,6},{4,8},{6,10},{8,12},{10,14},{12,0},{14,2},{1,5},{3,7},... | collective-permute-start | bytes 786440 | tf_op jit(solution)/shard_map/ppermute | solution.py:328
  10.2 1.1 %collective-permute-start.6 = (bf16[512,256]{1,0:T(8,128)(2,1)S(1)}, bf16[512,256]{1,0:T(8,128)(2,1)S(1)}, u32[]{:S(2)}, u32[]{:S(2)}) collective-permute-start(bf16[512,256]{1,0:T(8,128)(2,1)S(1)} %broadcast_select_fusion.3), channel_id=1, source_target_pairs={{0,2},{2,0},{4,6},{6,4},{8,10},{10,8},{12,14},{14,12},{1,3},{3,1},... | collective-permute-start | bytes 786440 | tf_op jit(solution)/shard_map/ppermute | solution.py:331
  11.3 4.1 %prompt_own.1 = (s32[11]{0:T(128)S(1)}, f32[2,8,256]{2,1,0:T(8,128)S(1)}, f32[2,8,256]{2,1,0:T(8,128)S(1)}, f32[2,1024,256]{2,1,0:T(8,128)S(1)}, bf16[2,2048,256]{2,1,0:T(8,128)(2,1)S(1)}) custom-call(s32[8]{0:T(128)} %win.1, s32[32,128]{1,0:T(8,128)} %bitcast.3, bf16[512,1024]{1,0:T(8,128)(2,1)} %q_ref.1, bf16[512,256]{1,0:T(8,128)(2,1)} %k_ref.1, ...), custom_call_target="tpu_custom_call" | custom-call | flops 300000000 | bytes 1048576 | tf_op jit(solution)/shard_map/prompt_own/pallas_call | solution.py:388
  15.5 0.5 collective-permute-start.7
  16.0 1.7 %collective-permute-start.4 = (bf16[512,256]{1,0:T(8,128)(2,1)S(1)}, bf16[512,256]{1,0:T(8,128)(2,1)S(1)}, u32[]{:S(2)}, u32[]{:S(2)}) collective-permute-start(bf16[512,256]{1,0:T(8,128)(2,1)S(1)} %collective-permute-done.2.refs_6_), channel_id=1, source_target_pairs={{0,4},{2,6},{4,8},{6,10},{8,12},{10,14},{12,0},{14,2},{1,5},{3,7},... | collective-permute-start | bytes 786440 | tf_op jit(solution)/shard_map/ppermute | solution.py:328
  17.8 2.3 %collective-permute-done.1.refs_5_ = bf16[512,256]{1,0:T(8,128)(2,1)S(1)} collective-permute-done((bf16[512,256]{1,0:T(8,128)(2,1)S(1)}, bf16[512,256]{1,0:T(8,128)(2,1)S(1)}, u32[]{:S(2)}, u32[]{:S(2)}) %collective-permute-start.1) | collective-permute-done | bytes 262176 | tf_op jit(solution)/shard_map/ppermute | solution.py:328
  20.1 0.4 collective-permute-start.8
  20.6 4.2 %prompt_far.3 = (f32[2,8,256]{2,1,0:T(8,128)S(1)}, f32[2,8,256]{2,1,0:T(8,128)S(1)}, f32[2,1024,256]{2,1,0:T(8,128)S(1)}) custom-call(s32[11]{0:T(128)S(1)} %get-tuple-element.30.refs_0_, bf16[2,2048,256]{2,1,0:T(8,128)(2,1)S(1)} %get-tuple-element.31.refs_1_, ...), custom_call_target="tpu_custom_call", output_to_operand_aliasing={{0}: (2, {}), {1}: (3, {}), {2}: (4, {})} | custom-call | flops 500000000 | bytes 1048576 | tf_op jit(solution)/shard_map/prompt_far/pallas_call | solution.py:406
  24.8 0.9 %collective-permute-done.4.refs_6_ = bf16[512,256]{1,0:T(8,128)(2,1)S(1)} collective-permute-done((bf16[512,256]{1,0:T(8,128)(2,1)S(1)}, bf16[512,256]{1,0:T(8,128)(2,1)S(1)}, u32[]{:S(2)}, u32[]{:S(2)}) %collective-permute-start.4) | collective-permute-done | bytes 262176 | tf_op jit(solution)/shard_map/ppermute | solution.py:328
  25.7 0.4 collective-permute-start.9
  26.2 2.7 %collective-permute-done.5.refs_1_ = bf16[288,256]{1,0:T(8,128)(2,1)S(1)} collective-permute-done((bf16[288,256]{1,0:T(8,128)(2,1)S(1)}, bf16[288,256]{1,0:T(8,128)(2,1)S(1)}, u32[]{:S(2)}, u32[]{:S(2)}) %collective-permute-start.5) | collective-permute-done | bytes 147488 | tf_op jit(solution)/shard_map/ppermute | solution.py:331
  29.0 2.6 %collective-permute-start.10 = (bf16[288,256]{1,0:T(8,128)(2,1)S(1)}, bf16[288,256]{1,0:T(8,128)(2,1)S(1)}, u32[]{:S(2)}, u32[]{:S(2)}) collective-permute-start(bf16[288,256]{1,0:T(8,128)(2,1)S(1)} %decode_merge.4.refs_0_), channel_id=1, source_target_pairs={{0,8},{2,10},{4,12},{6,14},{8,0},{10,2},{12,4},{14,6},{1,9},{3,11}... | collective-permute-start | bytes 442376 | tf_op jit(solution)/shard_map/ppermute | solution.py:331
  31.6 3.9 %prompt_far.4 = (f32[2,8,256]{2,1,0:T(8,128)S(1)}, f32[2,8,256]{2,1,0:T(8,128)S(1)}, f32[2,1024,256]{2,1,0:T(8,128)S(1)}) custom-call(s32[11]{0:T(128)S(1)} %get-tuple-element.30.refs_0_, bf16[2,2048,256]{2,1,0:T(8,128)(2,1)S(1)} %get-tuple-element.31.refs_1_, ...), custom_call_target="tpu_custom_call", output_to_operand_aliasing={{0}: (2, {}), {1}: (3, {}), {2}: (4, {})} | custom-call | flops 500000000 | bytes 1048576 | tf_op jit(solution)/shard_map/prompt_far/pallas_call | solution.py:406
  35.5 0.1 decode_merge.5.refs_1_.d_ref
  35.7 8.1 %prompt_far.5 = (f32[2,8,256]{2,1,0:T(8,128)S(1)}, f32[2,8,256]{2,1,0:T(8,128)S(1)}, f32[2,1024,256]{2,1,0:T(8,128)S(1)}, bf16[512,1024]{1,0:T(8,128)(2,1)S(1)}) custom-call(s32[11]{0:T(128)S(1)} %get-tuple-element.30.refs_0_, bf16[2,2048,256]{2,1,0:T(8,128)(2,1)S(1)} %get-tuple-element.31.refs_1_, ...), custom_call_target="tpu_custom_call", output_to_operand_aliasing={{0}: (2, {}), {1}: (3, {}), {2}: (4, {})} | custom-call | flops 500000000 | bytes 1048576 | tf_op jit(solution)/shard_map/prompt_far/pallas_call | solution.py:406
  43.9 1.4 %project_theirs.2 = bf16[288,2048]{1,0:T(8,128)(2,1)S(1)} custom-call(bf16[512,1024]{1,0:T(8,128)(2,1)S(1)} %get-tuple-element.48.refs_0_.a_ref, bf16[64,1024]{1,0:T(8,128)(2,1)S(1)} %decode_merge.5.refs_1_.d_ref, bf16[1024,4096]{1,0:T(8,128)(2,1)S(1)} %bitcast.2), custom_call_target="tpu_custom_call" | custom-call | flops 200000000 | bytes 1048576 | tf_op jit(solution)/shard_map/project_theirs/pallas_call | solution.py:476
  45.3 4.4 %collective-permute-start.11 = (bf16[288,2048]{1,0:T(8,128)(2,1)S(1)}, bf16[288,2048]{1,0:T(8,128)(2,1)S(1)}, u32[]{:S(2)}, u32[]{:S(2)}) collective-permute-start(bf16[288,2048]{1,0:T(8,128)(2,1)S(1)} %project_theirs.2), channel_id=1, source_target_pairs={{0,1},{1,0},{2,3},{3,2},{4,5},{5,4},{6,7},{7,6},{8,9},{9,8},{10,11... | collective-permute-start | bytes 3538952 | tf_op jit(solution)/shard_map/ppermute | solution.py:489
  49.6 1.4 %project_theirs.3 = bf16[288,2048]{1,0:T(8,128)(2,1)S(1)} custom-call(bf16[512,1024]{1,0:T(8,128)(2,1)S(1)} %get-tuple-element.48.refs_0_.a_ref, bf16[64,1024]{1,0:T(8,128)(2,1)S(1)} %decode_merge.5.refs_1_.d_ref, bf16[1024,4096]{1,0:T(8,128)(2,1)S(1)} %bitcast.2), custom_call_target="tpu_custom_call" | custom-call | flops 200000000 | bytes 1048576 | tf_op jit(solution)/shard_map/project_theirs/pallas_call | solution.py:476
  51.1 1.4 %project_own.1.mine_ref = bf16[288,2048]{1,0:T(8,128)(2,1)S(1)} custom-call(bf16[512,1024]{1,0:T(8,128)(2,1)S(1)} %get-tuple-element.48.refs_0_.a_ref, bf16[64,1024]{1,0:T(8,128)(2,1)S(1)} %decode_merge.5.refs_1_.d_ref, bf16[1024,4096]{1,0:T(8,128)(2,1)S(1)} %bitcast.2), custom_call_target="tpu_custom_call" | custom-call | flops 200000000 | bytes 1048576 | tf_op jit(solution)/shard_map/project_own/pallas_call | solution.py:476
  52.5 2.8 %project_early.1 = (bf16[256,4096]{1,0:T(8,128)(2,1)}, bf16[32,4096]{1,0:T(8,128)(2,1)}, bf16[288,2048]{1,0:T(8,128)(2,1)S(1)}) custom-call(bf16[512,1024]{1,0:T(8,128)(2,1)S(1)} %get-tuple-element.48.refs_0_.a_ref, bf16[64,1024]{1,0:T(8,128)(2,1)S(1)} %decode_merge.5.refs_1_.d_ref, bf16[1024,4096]{1,0:T(8,128)(2,1)S(1)} %bitcast.2, ...), custom_call_target="tpu_custom_call" | custom-call | flops 200000000 | bytes 1048576 | tf_op jit(solution)/shard_map/project_early/pallas_call | solution.py:495
  55.3 1.2 %project_late.1 = (bf16[256,4096]{1,0:T(8,128)(2,1)}, bf16[32,4096]{1,0:T(8,128)(2,1)}) custom-call(bf16[288,2048]{1,0:T(8,128)(2,1)S(1)} %get-tuple-element.51.mine_ref, bf16[288,2048]{1,0:T(8,128)(2,1)S(1)} %collective-permute-done.12.r_ref, bf16[256,4096]{1,0:T(8,128)(2,1)} %get-tuple-element.52._po, ...), custom_call_target="tpu_custom_call", output_to_operand_aliasing={{0}: (2, {}), {1}: (3, {})} | custom-call | flops 100000000 | bytes 1048576 | tf_op jit(solution)/shard_map/project_late/pallas_call | solution.py:506
  (30 shorter events, 0.5 us)
Async XLA Ops:
  0.6 9.6 %copy-start = (bf16[512,256]{1,0:T(8,128)(2,1)S(1)}, bf16[512,256]{1,0:T(8,128)(2,1)}, u32[]{:S(2)}) copy-start(bf16[512,256]{1,0:T(8,128)(2,1)} %k_ref.1) | copy-start | bytes 786436
  0.6 7.1 %copy-start.1 = (bf16[512,256]{1,0:T(8,128)(2,1)S(1)}, bf16[512,256]{1,0:T(8,128)(2,1)}, u32[]{:S(2)}) copy-start(bf16[512,256]{1,0:T(8,128)(2,1)} %v_ref.1) | copy-start | bytes 786436
  0.7 8.2 %collective-permute-start = (bf16[512,256]{1,0:T(8,128)(2,1)}, bf16[512,256]{1,0:T(8,128)(2,1)S(1)}, u32[]{:S(2)}, u32[]{:S(2)}) collective-permute-start(bf16[512,256]{1,0:T(8,128)(2,1)} %k_ref.1), channel_id=1, source_target_pairs={{0,4},{2,6},{4,8},{6,10},{8,12},{10,14},{12,0},{14,2},{1,5},{3,7},... | collective-permute-start | bytes 786440 | tf_op jit(solution)/shard_map/ppermute | solution.py:328
  6.4 9.0 %copy-start.2 = (bf16[512,256]{1,0:T(8,128)(2,1)S(1)}, bf16[512,256]{1,0:T(8,128)(2,1)}, u32[]{:S(2)}) copy-start(bf16[512,256]{1,0:T(8,128)(2,1)} %v_ref.1) | copy-start | bytes 786436
  6.4 11.2 %collective-permute-start.3 = (bf16[288,256]{1,0:T(8,128)(2,1)S(1)}, bf16[288,256]{1,0:T(8,128)(2,1)S(1)}, u32[]{:S(2)}, u32[]{:S(2)}) collective-permute-start(bf16[288,256]{1,0:T(8,128)(2,1)S(1)} %decode_pages.1.refs_0_), channel_id=1, source_target_pairs={{0,2},{2,0},{4,6},{6,4},{8,10},{10,8},{12,14},{14,12},{1,3},{3,1},... | collective-permute-start | bytes 442376 | tf_op jit(solution)/shard_map/ppermute | solution.py:331
  7.7 7.7 %collective-permute-start.2 = (bf16[512,256]{1,0:T(8,128)(2,1)S(1)}, bf16[512,256]{1,0:T(8,128)(2,1)S(1)}, u32[]{:S(2)}, u32[]{:S(2)}) collective-permute-start(bf16[512,256]{1,0:T(8,128)(2,1)S(1)} %copy-done.1), channel_id=1, source_target_pairs={{0,4},{2,6},{4,8},{6,10},{8,12},{10,14},{12,0},{14,2},{1,5},{3,7},... | collective-permute-start | bytes 786440 | tf_op jit(solution)/shard_map/ppermute | solution.py:328
  8.9 11.2 %collective-permute-start.1 = (bf16[512,256]{1,0:T(8,128)(2,1)S(1)}, bf16[512,256]{1,0:T(8,128)(2,1)S(1)}, u32[]{:S(2)}, u32[]{:S(2)}) collective-permute-start(bf16[512,256]{1,0:T(8,128)(2,1)S(1)} %collective-permute-done.refs_5_), channel_id=1, source_target_pairs={{0,4},{2,6},{4,8},{6,10},{8,12},{10,14},{12,0},{14,2},{1,5},{3,7},... | collective-permute-start | bytes 786440 | tf_op jit(solution)/shard_map/ppermute | solution.py:328
  10.2 21.3 %collective-permute-start.6 = (bf16[512,256]{1,0:T(8,128)(2,1)S(1)}, bf16[512,256]{1,0:T(8,128)(2,1)S(1)}, u32[]{:S(2)}, u32[]{:S(2)}) collective-permute-start(bf16[512,256]{1,0:T(8,128)(2,1)S(1)} %broadcast_select_fusion.3), channel_id=1, source_target_pairs={{0,2},{2,0},{4,6},{6,4},{8,10},{10,8},{12,14},{14,12},{1,3},{3,1},... | collective-permute-start | bytes 786440 | tf_op jit(solution)/shard_map/ppermute | solution.py:331
  15.5 16.1 %collective-permute-start.7 = (bf16[512,256]{1,0:T(8,128)(2,1)S(1)}, bf16[512,256]{1,0:T(8,128)(2,1)S(1)}, u32[]{:S(2)}, u32[]{:S(2)}) collective-permute-start(bf16[512,256]{1,0:T(8,128)(2,1)S(1)} %broadcast_select_fusion.2), channel_id=1, source_target_pairs={{0,2},{2,0},{4,6},{6,4},{8,10},{10,8},{12,14},{14,12},{1,3},{3,1},... | collective-permute-start | bytes 786440 | tf_op jit(solution)/shard_map/ppermute | solution.py:331
  16.0 9.7 %collective-permute-start.4 = (bf16[512,256]{1,0:T(8,128)(2,1)S(1)}, bf16[512,256]{1,0:T(8,128)(2,1)S(1)}, u32[]{:S(2)}, u32[]{:S(2)}) collective-permute-start(bf16[512,256]{1,0:T(8,128)(2,1)S(1)} %collective-permute-done.2.refs_6_), channel_id=1, source_target_pairs={{0,4},{2,6},{4,8},{6,10},{8,12},{10,14},{12,0},{14,2},{1,5},{3,7},... | collective-permute-start | bytes 786440 | tf_op jit(solution)/shard_map/ppermute | solution.py:328
  17.7 11.1 %collective-permute-start.5 = (bf16[288,256]{1,0:T(8,128)(2,1)S(1)}, bf16[288,256]{1,0:T(8,128)(2,1)S(1)}, u32[]{:S(2)}, u32[]{:S(2)}) collective-permute-start(bf16[288,256]{1,0:T(8,128)(2,1)S(1)} %decode_merge.3.refs_0_), channel_id=1, source_target_pairs={{0,4},{2,6},{4,0},{6,2},{8,12},{10,14},{12,8},{14,10},{1,5},{3,7},... | collective-permute-start | bytes 442376 | tf_op jit(solution)/shard_map/ppermute | solution.py:331
  20.1 15.5 %collective-permute-start.8 = (bf16[512,256]{1,0:T(8,128)(2,1)S(1)}, bf16[512,256]{1,0:T(8,128)(2,1)S(1)}, u32[]{:S(2)}, u32[]{:S(2)}) collective-permute-start(bf16[512,256]{1,0:T(8,128)(2,1)S(1)} %broadcast_select_fusion.1), channel_id=1, source_target_pairs={{0,2},{2,0},{4,6},{6,4},{8,10},{10,8},{12,14},{14,12},{1,3},{3,1},... | collective-permute-start | bytes 786440 | tf_op jit(solution)/shard_map/ppermute | solution.py:331
  20.6 23.3 %slice-start = ((s8[8388608]{0:T(1024)(128)(4,1)}), s8[4194304]{0:T(1024)(128)(4,1)S(1)}, s32[]{:S(2)}) async-start(s8[8388608]{0:T(1024)(128)(4,1)} %bitcast.1), calls=%async_computation | async-start | bytes 8388608
  25.7 9.9 %collective-permute-start.9 = (bf16[512,256]{1,0:T(8,128)(2,1)S(1)}, bf16[512,256]{1,0:T(8,128)(2,1)S(1)}, u32[]{:S(2)}, u32[]{:S(2)}) collective-permute-start(bf16[512,256]{1,0:T(8,128)(2,1)S(1)} %broadcast_select_fusion), channel_id=1, source_target_pairs={{0,2},{2,0},{4,6},{6,4},{8,10},{10,8},{12,14},{14,12},{1,3},{3,1},... | collective-permute-start | bytes 786440 | tf_op jit(solution)/shard_map/ppermute | solution.py:331
  29.0 6.6 %collective-permute-start.10 = (bf16[288,256]{1,0:T(8,128)(2,1)S(1)}, bf16[288,256]{1,0:T(8,128)(2,1)S(1)}, u32[]{:S(2)}, u32[]{:S(2)}) collective-permute-start(bf16[288,256]{1,0:T(8,128)(2,1)S(1)} %decode_merge.4.refs_0_), channel_id=1, source_target_pairs={{0,8},{2,10},{4,12},{6,14},{8,0},{10,2},{12,4},{14,6},{1,9},{3,11}... | collective-permute-start | bytes 442376 | tf_op jit(solution)/shard_map/ppermute | solution.py:331
  31.6 12.3 %slice-start.1 = ((s8[8388608]{0:T(1024)(128)(4,1)}), s8[4194304]{0:T(1024)(128)(4,1)S(1)}, s32[]{:S(2)}) async-start(s8[8388608]{0:T(1024)(128)(4,1)} %bitcast.1), calls=%async_computation.1 | async-start | bytes 8388608
  45.3 7.3 %collective-permute-start.11 = (bf16[288,2048]{1,0:T(8,128)(2,1)S(1)}, bf16[288,2048]{1,0:T(8,128)(2,1)S(1)}, u32[]{:S(2)}, u32[]{:S(2)}) collective-permute-start(bf16[288,2048]{1,0:T(8,128)(2,1)S(1)} %project_theirs.2), channel_id=1, source_target_pairs={{0,1},{1,0},{2,3},{3,2},{4,5},{5,4},{6,7},{7,6},{8,9},{9,8},{10,11... | collective-permute-start | bytes 3538952 | tf_op jit(solution)/shard_map/ppermute | solution.py:489
  51.0 4.2 %collective-permute-start.12 = (bf16[288,2048]{1,0:T(8,128)(2,1)S(1)}, bf16[288,2048]{1,0:T(8,128)(2,1)S(1)}, u32[]{:S(2)}, u32[]{:S(2)}) collective-permute-start(bf16[288,2048]{1,0:T(8,128)(2,1)S(1)} %project_theirs.3), channel_id=1, source_target_pairs={{0,1},{1,0},{2,3},{3,2},{4,5},{5,4},{6,7},{7,6},{8,9},{9,8},{10,11... | collective-permute-start | bytes 3538952 | tf_op jit(solution)/shard_map/ppermute | solution.py:489
